TPU v7x, 32 devices: a whole 2x2x4 slice. The times are simulated.
32 devices in a mesh: dp: 2 (over x), expert: 8 (over z, core), tensor: 2 (over y).
Axes of the slice: x: 2, y: 2, z: 4, core: 2. Of those that a mesh axis runs over, the one named last changes fastest.
Arguments:
- tokens: bfloat16 [192, 256, 1280], P(('dp', 'expert', 'tensor')), may hold values from -16 to 16
- cotangent: bfloat16 [192, 256, 1280], P(('dp', 'expert', 'tensor')), may hold values from -6 to 6
- norm_gain: float32 [1280], replicated, may hold values from 0.5 to 1.5
- slot_keys: bfloat16 [1280, 16], replicated, may hold values from -2 to 2
- w_in: bfloat16 [8, 1280, 2560], P('expert', None, 'tensor'), may hold values from -0.15625 to 0.15625
- w_out: bfloat16 [8, 2560, 1280], P('expert', 'tensor'), may hold values from -0.125 to 0.125
Outputs:
- grad_tokens: bfloat16 [192, 256, 1280], P(('dp', 'expert', 'tensor'))
- grad_gain: float32 [1280], replicated
- grad_keys: float32 [1280, 16], replicated
- grad_in: bfloat16 [8, 1280, 2560], P('expert', 'dp', 'tensor')
- grad_out: bfloat16 [8, 2560, 1280], P('expert', 'tensor', 'dp')
All inputs are finite; a program needn't handle non-finite values.
Results may differ from a plain program's by a relative error of at most 0.014.
The roundings to bfloat16 on the way count: a program that leaves them out, or rounds other values in their place, can miss the bound.
Values may be sent and summed in bfloat16 or wider, within the bound.
A program may use at most 128 MiB of HBM per device.

v0:
```python
import jax
import jax.numpy as jnp
from jax import lax
from jax.experimental import pallas as pl
from jax.experimental.pallas import tpu as pltpu
import functools
import numpy as np
from jax.sharding import PartitionSpec as P

SLOT_PER = 2


EPSILON = 1e-06


CHUNK = 64


def mix_kernel(x, c, gain, keys, perm, normed, disp, comb, stat, blk, stack):
    b = pl.program_id(0)
    slots = keys.shape[0]
    images = pl.num_programs(0)
    gains = gain[...]

    def rows_of(n, carry):
        rows = pl.ds(pl.multiple_of(n * CHUNK, CHUNK), CHUNK)
        values = x[0, rows, :].astype(jnp.float32)
        average = jnp.mean(values, axis=-1, keepdims=True)
        centred = values - average
        inverse = lax.rsqrt(jnp.mean(centred * centred, axis=-1, keepdims=True) + EPSILON)
        normed[0, rows, :] = (centred * inverse * gains).astype(jnp.bfloat16)
        lane = lax.broadcasted_iota(jnp.int32, (CHUNK, stat.shape[2]), 1)
        stat[0, rows, :] = jnp.where(lane == 0, average, inverse)
        return carry

    lax.fori_loop(0, x.shape[1] // CHUNK, rows_of, 0)
    logits = contract_cols(keys[...], normed[0])
    over_tokens = jnp.exp(logits - jnp.max(logits, axis=1, keepdims=True))
    over_tokens = over_tokens / jnp.sum(over_tokens, axis=1, keepdims=True)
    over_slots = jnp.exp(logits - jnp.max(logits, axis=0, keepdims=True))
    over_slots = over_slots / jnp.sum(over_slots, axis=0, keepdims=True)
    disp[0] = over_tokens
    comb[0] = over_slots
    start = pl.multiple_of(b * slots, slots)
    stack[0, pl.ds(start, slots), :] = jnp.dot(
        over_tokens.astype(jnp.bfloat16), normed[0], preferred_element_type=jnp.float32
    ).astype(jnp.bfloat16)
    stack[1, pl.ds(start, slots), :] = jnp.dot(
        over_slots.astype(jnp.bfloat16), c[0], preferred_element_type=jnp.float32
    ).astype(jnp.bfloat16)

    @pl.when(b == images - 1)
    def _():
        height = blk.shape[1]
        count = stack.shape[1]
        moved = jnp.dot(perm[:, 0:count], stack[0], preferred_element_type=jnp.float32)
        moved = moved + jnp.dot(perm[:, count:2 * count], stack[1], preferred_element_type=jnp.float32)
        for n in range(blk.shape[0]):
            blk[n] = moved[n * height:(n + 1) * height].astype(jnp.bfloat16)


def placement(images, experts):
    slots = experts * SLOT_PER
    height = 2 * images * SLOT_PER
    r = np.arange(experts * height)
    e, q = r // height, r % height
    stream, u = q // (images * SLOT_PER), q % (images * SLOT_PER)
    return stream, u // SLOT_PER, e * SLOT_PER + u % SLOT_PER, slots


def mix(tokens, cotangent, gain, keys, experts):
    images, count, features = tokens.shape
    stream, image, slot, slots = placement(images, experts)
    perm = np.zeros((stream.size, stream.size), np.float32)
    perm[np.arange(stream.size), stream * images * slots + image * slots + slot] = 1.0
    height = 2 * images * SLOT_PER
    per_image = lambda *tail: pl.BlockSpec((1,) + tail, lambda b: (b, 0, 0))
    whole = lambda *shape: pl.BlockSpec(shape, lambda b: (0,) * len(shape))
    low, wide = jnp.bfloat16, jnp.float32
    return pl.pallas_call(
        mix_kernel,
        grid=(images,),
        out_shape=(
            jax.ShapeDtypeStruct(tokens.shape, low),
            jax.ShapeDtypeStruct((images, slots, count), wide),
            jax.ShapeDtypeStruct((images, slots, count), wide),
            jax.ShapeDtypeStruct((images, count, 128), wide),
            jax.ShapeDtypeStruct((experts, height, features), low),
        ),
        in_specs=[
            per_image(count, features), per_image(count, features), whole(1, features),
            whole(slots, features), whole(*perm.shape),
        ],
        out_specs=(
            per_image(count, features), per_image(slots, count), per_image(slots, count),
            per_image(count, 128), whole(experts, height, features),
        ),
        scratch_shapes=[pltpu.VMEM((2, images * slots, features), low)],
        compiler_params=pltpu.CompilerParams(vmem_limit_bytes=32 * 1024 * 1024),
        name="mix",
    )(tokens, cotangent, gain, keys, jnp.asarray(perm, low))


def unmix_kernel(x, c, normed, disp, comb, stat, gain, keys, sel, back, out, gain_out, keys_out,
                 grad, gain_sum):
    b = pl.program_id(0)
    slots = keys.shape[0]
    low = jnp.bfloat16
    got = jnp.dot(sel[0], back[...], preferred_element_type=jnp.float32).astype(low)
    returned, slot_grad = got[0:slots], got[slots:2 * slots]
    grad_dispatch = contract_cols(slot_grad, normed[0])
    grad_combine = contract_cols(returned, c[0])
    dispatch, combine = disp[0], comb[0]
    logit = dispatch * (
        grad_dispatch - jnp.sum(dispatch * grad_dispatch, axis=1, keepdims=True)
    ) + combine * (grad_combine - jnp.sum(combine * grad_combine, axis=0, keepdims=True))
    first = logit.astype(low)
    rest = logit - first.astype(jnp.float32)
    second = rest.astype(low)
    third = (rest - second.astype(jnp.float32)).astype(low)
    key = keys[...]
    left = jnp.concatenate([dispatch.astype(low), first, second, third], axis=0)
    right = jnp.concatenate([slot_grad, key, key, key], axis=0)
    grad[...] = contract_rows(left, right)
    parts = jnp.dot(left[slots:], normed[0], preferred_element_type=jnp.float32)
    keys_here = parts[0:slots] + parts[slots:2 * slots] + parts[2 * slots:3 * slots]

    @pl.when(b == 0)
    def _():
        keys_out[...] = jnp.zeros_like(keys_out)
        gain_sum[...] = jnp.zeros_like(gain_sum)

    keys_out[...] += keys_here
    gains = gain[...]

    def rows_of(n, total):
        rows = pl.ds(pl.multiple_of(n * CHUNK, CHUNK), CHUNK)
        average, inverse = stat[0, rows, 0:1], stat[0, rows, 1:2]
        scaled = (x[0, rows, :].astype(jnp.float32) - average) * inverse
        grads = grad[rows, :]
        product = grads * scaled
        total = total + sum(product[k:k + 8] for k in range(0, CHUNK, 8))
        grads = grads * gains
        first_mean = jnp.mean(grads, axis=-1, keepdims=True)
        second_mean = jnp.mean(product * gains, axis=-1, keepdims=True)
        change = inverse * (grads - first_mean - scaled * second_mean)
        out[0, rows, :] = (c[0, rows, :].astype(jnp.float32) + change).astype(low)
        return total

    gain_sum[...] = lax.fori_loop(0, x.shape[1] // CHUNK, rows_of, gain_sum[...])

    @pl.when(b == pl.num_programs(0) - 1)
    def _():
        gain_out[...] = jnp.sum(gain_sum[...], axis=0, keepdims=True)


def unmix(tokens, cotangent, saved, gain, keys, back, experts):
    images, count, features = tokens.shape
    stream, image, slot, slots = placement(images, experts)
    sel = np.zeros((images, 2 * slots, stream.size), np.float32)
    sel[image, stream * slots + slot, np.arange(stream.size)] = 1.0
    normed, disp, comb, stat = saved
    per_image = lambda *tail: pl.BlockSpec((1,) + tail, lambda b: (b, 0, 0))
    whole = lambda *shape: pl.BlockSpec(shape, lambda b: (0,) * len(shape))
    return pl.pallas_call(
        unmix_kernel,
        grid=(images,),
        out_shape=(
            jax.ShapeDtypeStruct(tokens.shape, jnp.bfloat16),
            jax.ShapeDtypeStruct((1, features), jnp.float32),
            jax.ShapeDtypeStruct((slots, features), jnp.float32),
        ),
        in_specs=[
            per_image(count, features), per_image(count, features), per_image(count, features),
            per_image(slots, count), per_image(slots, count), per_image(count, 128),
            whole(1, features), whole(slots, features),
            per_image(2 * slots, stream.size), whole(stream.size, features),
        ],
        out_specs=(per_image(count, features), whole(1, features), whole(slots, features)),
        scratch_shapes=[
            pltpu.VMEM((count, features), jnp.float32), pltpu.VMEM((8, features), jnp.float32),
        ],
        compiler_params=pltpu.CompilerParams(vmem_limit_bytes=32 * 1024 * 1024),
        name="unmix",
    )(tokens, cotangent, normed, disp, comb, stat, gain, keys, jnp.asarray(sel, jnp.bfloat16), back)


def contract_rows(left, right):
    return lax.dot_general(
        left, right, (((0,), (0,)), ((), ())), preferred_element_type=jnp.float32
    )


def contract_cols(left, right):
    return lax.dot_general(
        left, right, (((1,), (1,)), ((), ())), preferred_element_type=jnp.float32
    )


MESH = pl.DeviceIdType.MESH
AXES = ("dp", "expert", "tensor")
GELU_A = 0.7978845608028654
GELU_B = 0.044715
TILE = 256


def gelu_of(x):
    return 0.5 * x * (1.0 + jnp.tanh(GELU_A * (x + GELU_B * (x * x * x))))


def gelu_slope(x):
    square = x * x
    bend = jnp.tanh(GELU_A * (x + GELU_B * (square * x)))
    return 0.5 * (1.0 + bend) + 0.5 * x * (1.0 - bend * bend) * (
        GELU_A * (1.0 + 3.0 * GELU_B * square)
    )


def experts_kernel(dp, experts, tensor, spread, finish, blk, w1, w2, back, *refs):
    if finish:
        grad_in, grad_out, turned, *refs = refs
    (s_all, g_all, h_all, p_all, rows, s32, g32, pre, part, sent, got, pair, ret,
     zs, zr, ys, yr, xs, xr, ps, pr, bs, br) = refs
    d, e, t = (lax.axis_index(name) for name in AXES)
    height = blk.shape[1]
    half = height // 2
    own = experts * half
    group = tensor * own
    width = blk.shape[2]
    units = w1.shape[1]

    def around(position, step, size):
        return lax.rem(position + (step + size), size)

    def push(src, dst, send, recv, axis, where):
        target = {"dp": d, "expert": e, "tensor": t}
        target[axis] = where
        return pltpu.make_async_remote_copy(
            src_ref=src, dst_ref=dst, send_sem=send, recv_sem=recv,
            device_id=tuple(target[name] for name in AXES), device_id_type=MESH,
        )

    barrier = pltpu.get_barrier_semaphore()
    peers = [("expert", e, experts), ("tensor", t, tensor)] + ([("dp", d, dp)] if spread > 1 else [])
    count = 0
    for axis, place, size in peers:
        for k in range(1, size):
            target = {"dp": d, "expert": e, "tensor": t}
            target[axis] = around(place, k, size)
            pl.semaphore_signal(barrier, inc=1, device_id=tuple(target[n] for n in AXES), device_id_type=MESH)
            count += 1
    pl.semaphore_wait(barrier, count)

    mine = d if spread > 1 else 0
    started = []

    def launch(copy):
        copy.start()
        started.append(copy)

    arrive = [None] * experts
    for k in sorted(range(1, experts), key=lambda k: -min(k, experts - k)):
        to = around(e, k, experts)
        arrive[k] = push(blk.at[to], rows.at[mine, t, e], zs.at[k], zr.at[k], "expert", to)
        launch(arrive[k])

    def spread_y(src, k):
        slot = rows.at[mine, t, around(e, -k, experts)]
        for j in range(1, tensor):
            launch(push(src, slot, ys.at[j, k], yr.at[j, k], "tensor", around(t, j, tensor)))

    def spread_x(src, j, k):
        if spread > 1:
            slot = rows.at[mine, around(t, -j, tensor), around(e, -k, experts)]
            for i in range(1, dp):
                launch(push(src, slot, xs.at[j, i, k], xr.at[j, i, k], "dp", around(d, i, dp)))

    spread_y(blk.at[e], 0)
    spread_x(blk.at[e], 0, 0)
    rows[mine, t, e] = blk[e]
    near = sorted(range(1, experts), key=lambda k: -min(k, experts - k))
    for k in near:
        arrive[k].wait_recv()
        slot = rows.at[mine, t, around(e, -k, experts)]
        spread_y(slot, k)
        spread_x(slot, 0, k)
    for k in [0] + near:
        for j in range(1, tensor):
            slot = rows.at[mine, around(t, -j, tensor), around(e, -k, experts)]
            push(slot, slot, ys.at[j, k], yr.at[j, k], "tensor", around(t, j, tensor)).wait_recv()
            spread_x(slot, j, k)

    def unpack(where, base):
        count = tensor * experts
        for n in range(count):
            s32[pl.ds(half * n, height), :] = rows[where, n // experts, n % experts].astype(jnp.float32)
        lead = (-half) % 8
        for n in reversed(range(count)):
            g32[pl.ds(half * n + lead, height), :] = rows[where, n // experts, n % experts].astype(jnp.float32)
        s_all[pl.ds(base, group), :] = s32[0:group, :].astype(jnp.bfloat16)
        g_all[pl.ds(base, group), :] = g32[half + lead:half + lead + group, :].astype(jnp.bfloat16)

    def forward(base):
        @pl.loop(0, units // TILE)
        def _(n):
            cols = pl.ds(pl.multiple_of(n * TILE, TILE), TILE)
            x = jnp.dot(s_all[pl.ds(base, group), :], w1[:, cols], preferred_element_type=jnp.float32)
            pre[:, cols] = x
            h_all[pl.ds(base, group), cols] = gelu_of(x).astype(jnp.bfloat16)

    def backward(base):
        @pl.loop(0, units // TILE)
        def _(n):
            cols = pl.ds(pl.multiple_of(n * TILE, TILE), TILE)
            x = contract_cols(g_all[pl.ds(base, group), :], w2[cols, :])
            p_all[pl.ds(base, group), cols] = (x * gelu_slope(pre[:, cols])).astype(jnp.bfloat16)

    def share(which):
        for j in range(1, tensor):
            to = around(t, j, tensor)
            sent[which, j - 1] = part[which, pl.ds(pl.multiple_of(to * own, 8), own), :].astype(jnp.bfloat16)
            launch(push(sent.at[which, j - 1], got.at[which, j - 1], ps.at[which, j], pr.at[which, j], "tensor", to))

    base = 0
    unpack(mine, base)
    forward(base)

    @pl.loop(0, width // TILE)
    def _(n):
        cols = pl.ds(pl.multiple_of(n * TILE, TILE), TILE)
        part[0, :, cols] = jnp.dot(h_all[0:group, :], w2[:, cols], preferred_element_type=jnp.float32)

    share(0)
    backward(base)

    @pl.loop(0, width // TILE)
    def _(n):
        cols = pl.ds(pl.multiple_of(n * TILE, TILE), TILE)
        part[1, :, cols] = contract_cols(p_all[0:group, :], w1[cols, :])

    share(1)
    for which in range(2):
        total = part[which, pl.ds(pl.multiple_of(t * own, 8), own), :]
        for j in range(1, tensor):
            push(got.at[which, j - 1], got.at[which, j - 1], ps.at[which, j], pr.at[which, j],
                 "tensor", around(t, j, tensor)).wait_recv()
            total = total + got[which, j - 1].astype(jnp.float32)
        (s32 if which == 0 else g32)[0:own, :] = total
    for n in range(experts):
        pair[0:half, :] = s32[half * n:half * n + half, :]
        pair[half:height, :] = g32[half * n:half * n + half, :]
        ret[n] = pair[...].astype(jnp.bfloat16)
    backs = []
    for k in near:
        to = around(e, k, experts)
        backs.append(push(ret.at[to], back.at[e], bs.at[k], br.at[k], "expert", to))
        launch(backs[-1])
    back[e] = ret[e]
    if spread > 1:
        for i in range(1, dp):
            other = around(d, -i, dp)
            for j in range(tensor):
                for k in range(experts):
                    slot = rows.at[other, around(t, -j, tensor), around(e, -k, experts)]
                    push(slot, slot, xs.at[j, i, k], xr.at[j, i, k], "dp", around(d, i, dp)).wait_recv()
            unpack(other, i * group)
            forward(i * group)
            backward(i * group)
    if finish:
        share_width = width // dp
        mine_cols = pl.ds(pl.multiple_of(d * share_width, 128), share_width)
        turned[...] = s_all[:, mine_cols].T

        @pl.loop(0, units // TILE)
        def _(n):
            cols = pl.ds(pl.multiple_of(n * TILE, TILE), TILE)
            grad_in[:, cols] = jnp.dot(
                turned[...], p_all[:, cols], preferred_element_type=jnp.float32
            ).astype(jnp.bfloat16)
            grad_out[cols, :] = contract_rows(h_all[:, cols], g_all[:, mine_cols]).astype(jnp.bfloat16)

    for copy in backs:
        copy.wait_recv()
    for copy in started:
        copy.wait_send()


def run_experts(blk, w1, w2, dp, experts, tensor):
    height, width = blk.shape[1:]
    units = w1.shape[1]
    spread = dp if dp <= 2 else 1
    group = tensor * experts * (height // 2)
    own = experts * (height // 2)
    total = spread * group
    low, wide = jnp.bfloat16, jnp.float32
    dma = pltpu.SemaphoreType.DMA
    vm = pl.BlockSpec(memory_space=pltpu.VMEM)
    shapes = [(total, width), (total, width), (total, units), (total, units)]
    finish = spread == dp and width % (128 * dp) == 0
    kept = [pltpu.VMEM(shape, low) for shape in shapes]
    if finish:
        shapes = [(width // dp, units), (units, width // dp)]
        kept = [pltpu.VMEM((width // dp, total), low)] + kept
    else:
        kept = []
    return pl.pallas_call(
        functools.partial(experts_kernel, dp, experts, tensor, spread, finish),
        out_shape=[jax.ShapeDtypeStruct(shape, low) for shape in [blk.shape] + shapes],
        in_specs=[vm] * 3,
        out_specs=[vm] * (1 + len(shapes)),
        scratch_shapes=kept + [
            pltpu.VMEM((spread, tensor, experts, height, width), low),
            pltpu.VMEM((group + 2 * height, width), wide),
            pltpu.VMEM((group + 2 * height, width), wide),
            pltpu.VMEM((group, units), wide),
            pltpu.VMEM((2, group, width), wide),
            pltpu.VMEM((2, max(tensor - 1, 1), own, width), low),
            pltpu.VMEM((2, max(tensor - 1, 1), own, width), low),
            pltpu.VMEM((height, width), wide),
            pltpu.VMEM((experts, height, width), low),
            dma((experts,)), dma((experts,)),
            dma((tensor, experts)), dma((tensor, experts)),
            dma((tensor, dp, experts)), dma((tensor, dp, experts)),
            dma((2, tensor)), dma((2, tensor)),
            dma((experts,)), dma((experts,)),
        ],
        compiler_params=pltpu.CompilerParams(
            collective_id=0, has_side_effects=True, vmem_limit_bytes=60 * 1024 * 1024
        ),
        name="experts",
    )(blk, w1, w2)


def reduce_kernel(sizes, x, out, got, total, ss, sr, gs, gr):
    where = [lax.axis_index(name) for name in AXES]
    table = [
        [place] + [lax.rem(place + k, size) for k in range(1, size)]
        for place, size in zip(where, sizes)
    ]
    targets = [(a, b, c) for a in table[0] for b in table[1] for c in table[2]]
    rank = lambda p: (p[0] * sizes[1] + p[1]) * sizes[2] + p[2]
    me = rank(where)
    others = range(1, len(targets))

    def scatter(k):
        return pltpu.make_async_remote_copy(
            src_ref=x.at[rank(targets[k])], dst_ref=got.at[k], send_sem=ss.at[k], recv_sem=sr.at[k],
            device_id=targets[k], device_id_type=MESH)

    def gather(k):
        return pltpu.make_async_remote_copy(
            src_ref=total, dst_ref=out.at[me], send_sem=gs.at[k], recv_sem=gr.at[k],
            device_id=targets[k], device_id_type=MESH)

    barrier = pltpu.get_barrier_semaphore()
    for k in others:
        pl.semaphore_signal(barrier, inc=1, device_id=targets[k], device_id_type=MESH)
    pl.semaphore_wait(barrier, len(others))
    first = [scatter(k) for k in others]
    for copy in first:
        copy.start()
    got[0] = x[me]
    for copy in first:
        copy.wait_recv()
    total[...] = jnp.sum(got[...], axis=0)
    second = [gather(k) for k in others]
    for copy in second:
        copy.start()
    out[me] = total[...]
    for copy in second:
        copy.wait_recv()
    for copy in first + second:
        copy.wait_send()


def reduce_all(values, sizes):
    count = sizes[0] * sizes[1] * sizes[2]
    flat = jnp.concatenate([v.reshape(-1) for v in values])
    chunk = -(-flat.shape[0] // (count * 1024)) * 1024
    packed = jnp.pad(flat, (0, count * chunk - flat.shape[0])).reshape(count, chunk // 128, 128)
    vm = pl.BlockSpec(memory_space=pltpu.VMEM)
    dma = pltpu.SemaphoreType.DMA
    summed = pl.pallas_call(
        functools.partial(reduce_kernel, sizes),
        out_shape=jax.ShapeDtypeStruct(packed.shape, jnp.float32),
        in_specs=[vm],
        out_specs=vm,
        scratch_shapes=[
            pltpu.VMEM(packed.shape, jnp.float32),
            pltpu.VMEM(packed.shape[1:], jnp.float32),
            dma((count,)), dma((count,)), dma((count,)), dma((count,)),
        ],
        compiler_params=pltpu.CompilerParams(collective_id=1, has_side_effects=True),
        name="reduce",
    )(packed).reshape(-1)
    results, start = [], 0
    for v in values:
        results.append(summed[start:start + v.size].reshape(v.shape))
        start += v.size
    return results


def local(sizes, tokens, cotangent, norm_gain, slot_keys, w_in, w_out):
    dp, experts, tensor = sizes
    features = tokens.shape[2]
    gain, keys = norm_gain.reshape(1, features), slot_keys.T
    *saved, blk = mix(tokens, cotangent, gain, keys, experts)
    back, *rest = run_experts(blk, w_in[0], w_out[0], dp, experts, tensor)
    if len(rest) == 2:
        first_total, second_total = rest
    else:
        slot_rows, grad_rows, hidden, grad_pre = rest
        if dp > 2:
            slot_rows = lax.all_to_all(slot_rows, "dp", split_axis=1, concat_axis=0, tiled=True)
            grad_rows = lax.all_to_all(grad_rows, "dp", split_axis=1, concat_axis=0, tiled=True)
            hidden = lax.all_gather(hidden, "dp", axis=0, tiled=True)
            grad_pre = lax.all_gather(grad_pre, "dp", axis=0, tiled=True)
        else:
            width = features // dp
            start = lax.axis_index("dp") * width
            slot_rows = lax.dynamic_slice_in_dim(slot_rows, start, width, axis=1)
            grad_rows = lax.dynamic_slice_in_dim(grad_rows, start, width, axis=1)
        first_total = contract_rows(slot_rows, grad_pre)
        second_total = contract_rows(hidden, grad_rows)
    grad_tokens, gain_term, keys_term = unmix(
        tokens, cotangent, saved, gain, keys, back.reshape(-1, features), experts
    )
    grad_gain, grad_keys = reduce_all((gain_term, keys_term), sizes)
    grad_gain, grad_keys = grad_gain.reshape(features), grad_keys.T
    return (
        grad_tokens,
        grad_gain,
        grad_keys,
        first_total.astype(jnp.bfloat16)[None],
        second_total.astype(jnp.bfloat16)[None],
    )


def solution(mesh):
    placed = (
        P(("dp", "expert", "tensor"), None, None),
        P(("dp", "expert", "tensor"), None, None),
        P(),
        P(),
        P("expert", None, "tensor"),
        P("expert", "tensor", None),
    )
    return jax.shard_map(
        functools.partial(local, tuple(mesh.shape[name] for name in AXES)),
        mesh=mesh,
        in_specs=placed,
        out_specs=(
            P(("dp", "expert", "tensor"), None, None),
            P(),
            P(),
            P("expert", "dp", "tensor"),
            P("expert", "tensor", "dp"),
        ),
        check_vma=False,
    )
```

profile of v0, /device:TPU:0, one launch (start us, length us, event | category | flops | bytes accessed | tf_op | source)
XLA Modules:
  0.0 128.5 jit_solution(14042274812784145703)
XLA Ops:
  0.6 0.7 reshape.31.gain
  1.3 2.1 %copy-done = bf16[6,256,1280]{2,1,0:T(8,128)(2,1)S(1)} copy-done((bf16[6,256,1280]{2,1,0:T(8,128)(2,1)S(1)}, bf16[6,256,1280]{2,1,0:T(8,128)(2,1)}, u32[]{:S(2)}) %copy-start) | copy-done | bytes 3932184
  3.4 2.1 %copy-done.2 = bf16[6,256,1280]{2,1,0:T(8,128)(2,1)S(1)} copy-done((bf16[6,256,1280]{2,1,0:T(8,128)(2,1)S(1)}, bf16[6,256,1280]{2,1,0:T(8,128)(2,1)}, u32[]{:S(2)}) %copy-start.2) | copy-done | bytes 3932184
  5.6 0.8 copy-done.10
  6.3 0.9 copy-done.17
  7.2 12.3 %mix.1 = (bf16[6,256,1280]{2,1,0:T(8,128)(2,1)S(1)}, f32[6,16,256]{2,1,0:T(8,128)S(1)}, f32[6,16,256]{2,1,0:T(8,128)S(1)}, f32[6,256,128]{2,1,0:T(8,128)S(1)}, bf16[8,24,1280]{2,1,0:T(8,128)(2,1)S(1)}) custom-call(bf16[6,256,1280]{2,1,0:T(8,128)(2,1)S(1)} %copy-done, bf16[6,256,1280]{2,1,0:T(8,128)(2,1)S(1)} %copy-done.2, f32[1,1280]{1,0:T(1,128)S(1)} %reshape.31.gain, ...), custom_call_target="tpu_custom_call" | custom-call | tf_op jit(solution)/shard_map/mix/pallas_call | solution.py:80
  19.6 1.9 %copy-done.4 = bf16[6,256,1280]{2,1,0:T(8,128)(2,1)} copy-done((bf16[6,256,1280]{2,1,0:T(8,128)(2,1)}, bf16[6,256,1280]{2,1,0:T(8,128)(2,1)S(1)}, u32[]{:S(2)}) %copy-start.4) | copy-done | bytes 3932184
  21.5 0.9 copy-done.6
  22.4 0.8 copy-done.9
  24.4 54.2 %experts.1 = (bf16[8,24,1280]{2,1,0:T(8,128)(2,1)}, bf16[640,1280]{1,0:T(8,128)(2,1)}, bf16[1280,640]{1,0:T(8,128)(2,1)}) custom-call(bf16[8,24,1280]{2,1,0:T(8,128)(2,1)} %copy-done.9, bf16[1280,1280]{1,0:T(8,128)(2,1)} %bitcast.13, bf16[1280,1280]{1,0:T(8,128)(2,1)} %bitcast.14), custom_call_target="tpu_custom_call" | custom-call | tf_op jit(solution)/shard_map/experts/pallas_call | solution.py:406
  78.7 2.1 %copy-done.3 = bf16[6,256,1280]{2,1,0:T(8,128)(2,1)S(1)} copy-done((bf16[6,256,1280]{2,1,0:T(8,128)(2,1)S(1)}, bf16[6,256,1280]{2,1,0:T(8,128)(2,1)}, u32[]{:S(2)}) %copy-start.3) | copy-done | bytes 3932184
  80.8 2.1 %copy-done.5 = bf16[6,256,1280]{2,1,0:T(8,128)(2,1)S(1)} copy-done((bf16[6,256,1280]{2,1,0:T(8,128)(2,1)S(1)}, bf16[6,256,1280]{2,1,0:T(8,128)(2,1)}, u32[]{:S(2)}) %copy-start.5) | copy-done | bytes 3932184
  83.0 1.1 copy-done.7
  84.1 1.0 copy-done.8
  85.1 0.9 copy-done.14
  86.0 0.9 copy-done.16
  86.9 13.2 %unmix.1 = (bf16[6,256,1280]{2,1,0:T(8,128)(2,1)}, f32[1,1280]{1,0:T(1,128)S(1)}, f32[16,1280]{1,0:T(8,128)S(1)}) custom-call(bf16[6,256,1280]{2,1,0:T(8,128)(2,1)S(1)} %copy-done.1, bf16[6,256,1280]{2,1,0:T(8,128)(2,1)S(1)} %copy-done.3, bf16[6,256,1280]{2,1,0:T(8,128)(2,1)S(1)} %copy-done.5, f32[6,16,256]{2,1,0:T(8,128)S(1)} %copy-done.14, ...), custom_call_target="tpu_custom_call" | custom-call | tf_op jit(solution)/shard_map/unmix/pallas_call | solution.py:165
  100.8 1.0 reshape.34
  101.8 0.7 fusion.x
  102.5 19.3 %reduce.2 = f32[32,8,128]{2,1,0:T(8,128)} custom-call(f32[32,8,128]{2,1,0:T(8,128)} %fusion.x), custom_call_target="tpu_custom_call" | custom-call | tf_op jit(solution)/shard_map/reduce/pallas_call | solution.py:483
  121.8 1.3 %slice.8 = f32[1280]{0:T(1024)} slice(f32[32768]{0:T(1024)} %bitcast.17), slice={[0:1280]} | slice | bytes 10240 | tf_op jit(solution)/shard_map/slice | solution.py:498
  123.1 0.9 slice.9
  124.6 2.7 %copy.15 = bf16[1,640,1280]{2,1,0:T(8,128)(2,1)} copy(bf16[1,640,1280]{2,1,0:T(8,128)(2,1)} %bitcast.16) | data formatting | bytes 3276800
  127.3 1.2 copy.16
  (29 shorter events, 2.6 us)
Async XLA Ops:
  1.3 2.1 %copy-start = (bf16[6,256,1280]{2,1,0:T(8,128)(2,1)S(1)}, bf16[6,256,1280]{2,1,0:T(8,128)(2,1)}, u32[]{:S(2)}) copy-start(bf16[6,256,1280]{2,1,0:T(8,128)(2,1)} %x.5) | copy-start | bytes 11796484
  3.4 2.1 %copy-start.2 = (bf16[6,256,1280]{2,1,0:T(8,128)(2,1)S(1)}, bf16[6,256,1280]{2,1,0:T(8,128)(2,1)}, u32[]{:S(2)}) copy-start(bf16[6,256,1280]{2,1,0:T(8,128)(2,1)} %c.3) | copy-start | bytes 11796484
  5.6 0.8 copy-start.10
  6.3 0.9 copy-start.17
  19.6 1.9 %copy-start.4 = (bf16[6,256,1280]{2,1,0:T(8,128)(2,1)}, bf16[6,256,1280]{2,1,0:T(8,128)(2,1)S(1)}, u32[]{:S(2)}) copy-start(bf16[6,256,1280]{2,1,0:T(8,128)(2,1)S(1)} %get-tuple-element.16.normed) | copy-start | bytes 11796484
  21.5 0.9 copy-start.6
  22.4 0.8 copy-start.9
  23.2 0.6 copy-start.13
  23.8 0.6 copy-start.15
  24.4 54.3 %copy-start.1 = (bf16[6,256,1280]{2,1,0:T(8,128)(2,1)S(1)}, bf16[6,256,1280]{2,1,0:T(8,128)(2,1)}, u32[]{:S(2)}) copy-start(bf16[6,256,1280]{2,1,0:T(8,128)(2,1)} %x.5) | copy-start | bytes 11796484
  24.4 54.3 %copy-start.11 = (bf16[1280,16]{0,1:T(8,128)(2,1)S(1)}, bf16[1280,16]{0,1:T(8,128)(2,1)}, u32[]{:S(2)}) copy-start(bf16[1280,16]{0,1:T(8,128)(2,1)} %param.11) | copy-start | bytes 122884
  24.4 54.3 %copy-start.12 = (bf16[6,32,192]{2,1,0:T(8,128)(2,1)S(1)}, bf16[6,32,192]{2,1,0:T(8,128)(2,1)}, u32[]{:S(2)}) copy-start(bf16[6,32,192]{2,1,0:T(8,128)(2,1)} %constant.8.clone.sel) | copy-start | bytes 221188
  78.7 2.1 %copy-start.3 = (bf16[6,256,1280]{2,1,0:T(8,128)(2,1)S(1)}, bf16[6,256,1280]{2,1,0:T(8,128)(2,1)}, u32[]{:S(2)}) copy-start(bf16[6,256,1280]{2,1,0:T(8,128)(2,1)} %c.3) | copy-start | bytes 11796484
  80.8 2.1 %copy-start.5 = (bf16[6,256,1280]{2,1,0:T(8,128)(2,1)S(1)}, bf16[6,256,1280]{2,1,0:T(8,128)(2,1)}, u32[]{:S(2)}) copy-start(bf16[6,256,1280]{2,1,0:T(8,128)(2,1)} %copy-done.4) | copy-start | bytes 11796484
  83.0 1.1 copy-start.7
  84.1 1.0 copy-start.8
  85.1 0.9 copy-start.14
  86.0 0.9 copy-start.16
  100.1 0.6 copy-start.18
  100.8 26.6 %copy-start.19 = (bf16[1280,640]{1,0:T(8,128)(2,1)S(1)}, bf16[1280,640]{1,0:T(8,128)(2,1)}, u32[]{:S(2)}) copy-start(bf16[1280,640]{1,0:T(8,128)(2,1)} %get-tuple-element.26) | copy-start | bytes 4915204
where the time goes:
time: 129 us; the launch traced here: 128 us
  Pallas kernels  99.1 us (77%)
  local copies, waits for them, and re-layouts  28 us (22%)
    pallas_call x1, Pallas kernels, run_experts(): pl.pallas_call(functools.partial(experts_kernel, dp, experts, tensor, spr...  54.2 us
    unnamed x42, local copies, waits for them, and re-layouts  23.4 us
    pallas_call x1, Pallas kernels, reduce_all(): pl.pallas_call(functools.partial(reduce_kernel, sizes), out_shape=jax.Sha...  19.3 us
    pallas_call x1, Pallas kernels, unmix(): pl.pallas_call(unmix_kernel, grid=(images,), out_shape=(jax.ShapeDtypeStr...  13.2 us
    pallas_call x1, Pallas kernels, mix(): pl.pallas_call(mix_kernel, grid=(images,), out_shape=(jax.ShapeDtypeStruc...  12.3 us

commit v1 on v0

v1 whole, which is shorter than its diff:
```python
import functools
import types

import jax
import jax.numpy as jnp
import numpy as np
from jax import lax
from jax.experimental import pallas as pl
from jax.experimental.pallas import tpu as pltpu
from jax.sharding import PartitionSpec as P

AXES = ("dp", "expert", "tensor")
MESH = pl.DeviceIdType.MESH
SLOT_PER = 2
EPSILON = 1e-06
GELU_A = 0.7978845608028654
GELU_B = 0.044715
TILE = 256
ROWS = 64
LOW, WIDE = jnp.bfloat16, jnp.float32


def contract_rows(left, right):
    return lax.dot_general(left, right, (((0,), (0,)), ((), ())), preferred_element_type=WIDE)


def contract_cols(left, right):
    return lax.dot_general(left, right, (((1,), (1,)), ((), ())), preferred_element_type=WIDE)


def gelu_of(x):
    return 0.5 * x * (1.0 + jnp.tanh(GELU_A * (x + GELU_B * (x * x * x))))


def gelu_slope(x):
    square = x * x
    bend = jnp.tanh(GELU_A * (x + GELU_B * (square * x)))
    return 0.5 * (1.0 + bend) + 0.5 * x * (1.0 - bend * bend) * (
        GELU_A * (1.0 + 3.0 * GELU_B * square)
    )


def around(position, step, size):
    return lax.rem(position + (step + size), size)


def tables(pair, experts, tensor):
    slots, quarter = experts * SLOT_PER, pair * SLOT_PER
    height, own = 2 * quarter, experts * quarter
    group = tensor * own

    def hot(source):
        table = np.zeros((source.size, source.size), np.float32)
        table[np.arange(source.size), source] = 1.0
        return jnp.asarray(table, LOW)

    r = np.arange(experts * height)
    e, stream, u = r // height, r % height // quarter, r % quarter
    image_order = stream * pair * slots + u // SLOT_PER * slots + e * SLOT_PER + u % SLOT_PER
    stream_order = stream * own + e * quarter + u
    r = np.arange(2 * group)
    block_order = r % group // quarter * height + r // group * quarter + r % quarter
    r = np.arange(experts * height)
    image, stream, slot = r // (2 * slots), r % (2 * slots) // slots, r % slots
    back_order = slot // SLOT_PER * height + stream * quarter + image * SLOT_PER + slot % SLOT_PER
    return hot(image_order), hot(block_order), hot(stream_order), hot(back_order)


def exchange_kernel(sizes, spread, names, *refs):
    dp, experts, tensor = sizes
    r = types.SimpleNamespace(**dict(zip(names, refs)))
    d, e, t = (lax.axis_index(name) for name in AXES)
    images, count, features = r.x.shape
    slots, units = r.keys.shape[0], r.w1.shape[1]
    chunks, _, height, _ = r.blk.shape
    pair, quarter = images // chunks, height // 2
    own = experts * quarter
    group = tensor * own
    lanes = features // 128
    mine = d if spread > 1 else 0
    where = [d, e, t]

    def push(src, dst, send, recv, axis, place):
        target = {"dp": d, "expert": e, "tensor": t}
        target[axis] = place
        return pltpu.make_async_remote_copy(
            src_ref=src, dst_ref=dst, send_sem=send, recv_sem=recv,
            device_id=tuple(target[name] for name in AXES), device_id_type=MESH,
        )

    started = []

    def launch(copy):
        copy.start()
        started.append(copy)

    offsets = [(a, b, c) for a in range(dp) for b in range(experts) for c in range(tensor)]
    targets = [tuple(around(w, k, s) for w, k, s in zip(where, step, sizes)) for step in offsets]
    sources = [tuple(around(w, -k, s) for w, k, s in zip(where, step, sizes)) for step in offsets]
    others = range(1, len(offsets))
    rank = lambda p: (p[0] * experts + p[1]) * tensor + p[2]

    fetched = []

    def fetch(src, dst):
        copy = pltpu.make_async_copy(src, dst, r.in_sem.at[len(fetched)])
        copy.start()
        fetched.append(copy)
        return copy

    def image_copy(b, n):
        return pltpu.make_async_copy(
            (r.x_in, r.c_in)[n].at[b], (r.x, r.c)[n].at[b], r.image_sem.at[n, b])

    image_copy(0, 0).start()
    small = [fetch(r.gain_in, r.gain_rows), fetch(r.keys_in, r.keys), fetch(r.mixes_in, r.mixes)]
    image_copy(0, 1).start()
    barrier = pltpu.get_barrier_semaphore()
    for k in others:
        pl.semaphore_signal(barrier, inc=1, device_id=targets[k], device_id_type=MESH)
    for b in range(1, images):
        image_copy(b, 0).start()
        image_copy(b, 1).start()
    unp_copy, ret_copy, sel_copy = (
        fetch(r.unp_in, r.unp), fetch(r.ret_in, r.turn), fetch(r.sel_in, r.sel))
    w1_copy, w2_copy = fetch(r.w1_in, r.w1), fetch(r.w2_in, r.w2)
    for copy in small:
        copy.wait()
    r.gains[...] = jnp.concatenate([r.gain_rows[n:n + 1, :] for n in range(lanes)], axis=1)
    r.keys_sum[...] = jnp.zeros_like(r.keys_sum)
    r.gain_sum[...] = jnp.zeros_like(r.gain_sum)

    def mix_image(b, slab):
        image_copy(b, 0).wait()
        gains = r.gains[...]

        def rows_of(n, carry):
            rows = pl.ds(pl.multiple_of(n * ROWS, ROWS), ROWS)
            values = r.x[b, rows, :].astype(WIDE)
            average = jnp.mean(values, axis=-1, keepdims=True)
            centred = values - average
            inverse = lax.rsqrt(jnp.mean(centred * centred, axis=-1, keepdims=True) + EPSILON)
            r.normed[b, rows, :] = (centred * inverse * gains).astype(LOW)
            lane = lax.broadcasted_iota(jnp.int32, (ROWS, 128), 1)
            r.stat[b, rows, :] = jnp.where(lane == 0, average, inverse)
            return carry

        lax.fori_loop(0, count // ROWS, rows_of, 0)
        logits = contract_cols(r.keys[...], r.normed[b])
        over_tokens = jnp.exp(logits - jnp.max(logits, axis=1, keepdims=True))
        over_tokens = over_tokens / jnp.sum(over_tokens, axis=1, keepdims=True)
        over_slots = jnp.exp(logits - jnp.max(logits, axis=0, keepdims=True))
        over_slots = over_slots / jnp.sum(over_slots, axis=0, keepdims=True)
        r.logits[b] = logits
        r.disp[b] = over_tokens
        r.comb[b] = over_slots
        image_copy(b, 1).wait()
        taken = jnp.dot(over_tokens.astype(LOW), r.normed[b], preferred_element_type=WIDE)
        given = jnp.dot(over_slots.astype(LOW), r.c[b], preferred_element_type=WIDE)
        r.slot_in[b] = taken
        start = pl.multiple_of(slab * slots, slots)
        r.stack[pl.ds(start, slots), :] = taken.astype(LOW)
        start = pl.multiple_of((pair + slab) * slots, slots)
        r.stack[pl.ds(start, slots), :] = given.astype(LOW)

    def mix(c):
        @pl.loop(0, pair)
        def _(slab):
            mix_image(c * pair + slab, slab)

        moved = jnp.dot(r.mixes[...], r.stack[...], preferred_element_type=WIDE)
        for n in range(experts):
            r.blk[c, n] = moved[n * height:(n + 1) * height].astype(LOW)

    near = sorted(range(1, experts), key=lambda k: -min(k, experts - k))
    arrive = {}

    def scatter(c):
        for k in near:
            to = around(e, k, experts)
            arrive[c, k] = push(r.blk.at[c, to], r.rows.at[c, mine, t, e],
                                r.zs.at[c, k], r.zr.at[c, k], "expert", to)
            launch(arrive[c, k])
        share_rows(c, r.blk.at[c, e], 0)
        r.rows[c, mine, t, e] = r.blk[c, e]

    def share_rows(c, src, k):
        slot = r.rows.at[c, mine, t, around(e, -k, experts)]
        for j in range(1, tensor):
            launch(push(src, slot, r.ys.at[c, j, k], r.yr.at[c, j, k], "tensor", around(t, j, tensor)))

    def share_slab(c, j):
        for i in range(1, spread):
            slab = r.rows.at[c, mine, around(t, -j, tensor)]
            launch(push(slab, slab, r.xs.at[c, j, i], r.xr.at[c, j, i], "dp", around(d, i, dp)))

    def forward_rows(c):
        for k in near:
            arrive[c, k].wait_recv()
            share_rows(c, r.rows.at[c, mine, t, around(e, -k, experts)], k)
        share_slab(c, 0)

    def gather_rows(c):
        for j in range(1, tensor):
            for k in [0] + near:
                slot = r.rows.at[c, mine, around(t, -j, tensor), around(e, -k, experts)]
                push(slot, slot, r.ys.at[c, j, k], r.yr.at[c, j, k],
                     "tensor", around(t, j, tensor)).wait_recv()
            share_slab(c, j)

    def unpack(c, place, base):
        block = r.rows[c, place].reshape(2 * group, features)
        both = jnp.dot(r.unp[...], block, preferred_element_type=WIDE)
        r.s_all[pl.ds(base, group), :] = both[0:group].astype(LOW)
        r.g_all[pl.ds(base, group), :] = both[group:].astype(LOW)

    def tiles(extent):
        def over(body):
            @pl.loop(0, extent // TILE)
            def _(n):
                body(pl.ds(pl.multiple_of(n * TILE, TILE), TILE))
        return over

    def forward(base, size):
        @tiles(units)
        def _(cols):
            x = jnp.dot(r.s_all[pl.ds(base, size), :], r.w1[:, cols], preferred_element_type=WIDE)
            r.pre[pl.ds(0, size), cols] = x
            r.h_all[pl.ds(base, size), cols] = gelu_of(x).astype(LOW)

    def backward(base, size):
        @tiles(units)
        def _(cols):
            x = contract_cols(r.g_all[pl.ds(base, size), :], r.w2[cols, :])
            r.p_all[pl.ds(base, size), cols] = (x * gelu_slope(r.pre[pl.ds(0, size), cols])).astype(LOW)

    def project(c, base):
        @tiles(features)
        def _(cols):
            r.part[c, 0, :, cols] = jnp.dot(
                r.h_all[pl.ds(base, group), :], r.w2[:, cols], preferred_element_type=WIDE)

        share_part(c, 0)

    def project_back(c, base):
        @tiles(features)
        def _(cols):
            r.part[c, 1, :, cols] = contract_cols(r.p_all[pl.ds(base, group), :], r.w1[cols, :])

        share_part(c, 1)

    def part_copy(c, which, j):
        return push(r.sent.at[c, which, j - 1], r.got.at[c, which, j - 1],
                    r.ps.at[c, which, j], r.pr.at[c, which, j], "tensor", around(t, j, tensor))

    def share_part(c, which):
        for j in range(1, tensor):
            to = around(t, j, tensor)
            r.sent[c, which, j - 1] = r.part[c, which, pl.ds(pl.multiple_of(to * own, 8), own), :].astype(LOW)
            launch(part_copy(c, which, j))

    def give_back(c):
        totals = []
        for which in range(2):
            total = r.part[c, which, pl.ds(pl.multiple_of(t * own, 8), own), :]
            for j in range(1, tensor):
                part_copy(c, which, j).wait_recv()
                total = total + r.got[c, which, j - 1].astype(WIDE)
            totals.append(total.astype(LOW))
        moved = jnp.dot(r.turn[...], jnp.concatenate(totals, axis=0), preferred_element_type=WIDE)
        for n in range(experts):
            r.ret[c, n] = moved[n * height:(n + 1) * height].astype(LOW)
        for k in near:
            to = around(e, k, experts)
            arrive["back", c, k] = push(r.ret.at[c, to], r.back.at[c, e],
                                        r.bs.at[c, k], r.br.at[c, k], "expert", to)
            launch(arrive["back", c, k])
        r.back[c, e] = r.ret[c, e]

    def image_gradients(b, slab):
        start = pl.multiple_of(slab * 2 * slots, 2 * slots)
        returned = r.found[pl.ds(start, slots), :]
        slot_grad = r.found[pl.ds(start + slots, slots), :]
        grad_dispatch = contract_cols(slot_grad, r.normed[b])
        grad_combine = contract_cols(returned, r.c[b])
        dispatch, combine = r.disp[b], r.comb[b]
        logit = dispatch * (
            grad_dispatch - jnp.sum(dispatch * grad_dispatch, axis=1, keepdims=True)
        ) + combine * (grad_combine - jnp.sum(combine * grad_combine, axis=0, keepdims=True))
        first = logit.astype(LOW)
        rest = logit - first.astype(WIDE)
        second = rest.astype(LOW)
        third = (rest - second.astype(WIDE)).astype(LOW)
        low = dispatch.astype(LOW)
        split = jnp.concatenate([first, second, third], axis=0)
        r.left[b, 0:slots, :] = low
        r.left[b, slots:4 * slots, :] = split
        r.right[b] = slot_grad
        parts = jnp.dot(split, r.normed[b], preferred_element_type=WIDE)
        r.keys_sum[...] += parts[0:slots] + parts[slots:2 * slots] + parts[2 * slots:3 * slots]
        wide = slot_grad.astype(WIDE)
        r.gain_sum[...] += wide * r.slot_in[b]
        low = low.astype(WIDE)
        gains = r.gains[...]
        from_slots = jnp.sum(wide * gains, axis=1, keepdims=True)
        from_keys = jnp.sum(r.keys[...].astype(WIDE) * gains, axis=1, keepdims=True)
        first_mean = jnp.sum(low * from_slots + logit * from_keys, axis=0, keepdims=True)
        second_mean = jnp.sum(low * grad_dispatch + logit * r.logits[b], axis=0, keepdims=True)
        row = lax.broadcasted_iota(jnp.int32, (8, count), 0)
        r.moment[b] = jnp.where(row == 0, first_mean, second_mean) * (1.0 / features)

    def take_back(c):
        for k in near:
            arrive["back", c, k].wait_recv()
        block = r.back[c].reshape(experts * height, features)
        r.found[...] = jnp.dot(r.sel[...], block, preferred_element_type=WIDE).astype(LOW)

        @pl.loop(0, pair)
        def _(slab):
            image_gradients(c * pair + slab, slab)

    placed = []

    def place_out(src, dst):
        copy = pltpu.make_async_copy(src, dst, r.out_sem.at[len(placed)])
        copy.start()
        placed.append(copy)

    for c in range(chunks):
        mix(c)
        if c == 0:
            pl.semaphore_wait(barrier, len(others))
        scatter(c)
    for copy in (unp_copy, ret_copy, sel_copy, w1_copy, w2_copy):
        copy.wait()
    place_out(r.stat, r.stat_out)
    forward_rows(0)
    for c in range(chunks):
        base = c * group
        gather_rows(c)
        unpack(c, mine, base)
        forward(base, group)
        if c > 0:
            give_back(c - 1)
        project(c, base)
        backward(base, group)
        if c + 1 < chunks:
            forward_rows(c + 1)
        project_back(c, base)
    full = chunks * group

    def other_rows(i):
        other = around(d, -i, dp)
        for c in range(chunks):
            for j in range(tensor):
                slab = r.rows.at[c, other, around(t, -j, tensor)]
                push(slab, slab, r.xs.at[c, j, i], r.xr.at[c, j, i], "dp", around(d, i, dp)).wait_recv()
            unpack(c, other, i * full + c * group)

    for i in range(1, spread):
        other_rows(i)
        forward(i * full, full)
    give_back(chunks - 1)
    for i in range(1, spread):
        backward(i * full, full)
    if r.s_out.shape[1] != features:
        part_cols = pl.ds(pl.multiple_of(d * r.s_out.shape[1], 128), r.s_out.shape[1])
    else:
        part_cols = slice(None)
    place_out(r.s_all.at[:, part_cols], r.s_out)
    place_out(r.g_all.at[:, part_cols], r.g_out)
    place_out(r.h_all, r.h_out)
    place_out(r.p_all, r.p_out)
    for c in range(chunks):
        take_back(c)
    place_out(r.left, r.left_out)
    place_out(r.right, r.right_out)
    place_out(r.moment, r.moment_out)

    each = r.pack.shape[1] // 8
    bands = slots // 8
    count_tiles = bands * lanes + -(-lanes // 8)
    owners = -(-count_tiles // each)
    me = rank(where)
    gain = jnp.sum(r.gain_sum[...] + r.keys[...].astype(WIDE) * r.keys_sum[...], axis=0, keepdims=True)
    gain = gain / r.gains[...]
    for n in range(bands * lanes):
        band, lane = n // lanes, n % lanes
        r.pack[n // each, pl.ds(n % each * 8, 8), :] = r.keys_sum[
            band * 8:band * 8 + 8, lane * 128:lane * 128 + 128]
    for n in range(-(-lanes // 8) * 8):
        m = bands * lanes + n // 8
        row = m % each * 8 + n % 8
        piece = gain[:, n * 128:n * 128 + 128] if n < lanes else jnp.zeros((1, 128), WIDE)
        r.pack[m // each, row:row + 1, :] = piece

    def reduce_copy(k):
        return pltpu.make_async_remote_copy(
            src_ref=r.pack.at[rank(targets[k])], dst_ref=r.heap.at[k], send_sem=r.ss.at[k],
            recv_sem=r.sr.at[k], device_id=targets[k], device_id_type=MESH)

    def spread_copy(k):
        return pltpu.make_async_remote_copy(
            src_ref=r.total, dst_ref=r.summed.at[me], send_sem=r.gs.at[k],
            recv_sem=r.gr.at[k], device_id=targets[k], device_id_type=MESH)

    def gated(test, action):
        pl.when(test)(action)

    for k in others:
        gated(rank(targets[k]) < owners, lambda k=k: reduce_copy(k).start())

    @pl.when(me < owners)
    def _():
        r.heap[0] = r.pack[me]
        for k in others:
            reduce_copy(k).wait_recv()
        r.total[...] = jnp.sum(r.heap[...], axis=0)
        for k in others:
            spread_copy(k).start()
        r.summed[me] = r.total[...]

    for k in others:
        gated(rank(sources[k]) < owners, lambda k=k: spread_copy(k).wait_recv())
    place_out(r.summed.at[pl.ds(0, owners)], r.summed_out)
    for copy in started:
        copy.wait_send()
    for k in others:
        gated(rank(targets[k]) < owners, lambda k=k: reduce_copy(k).wait_send())

    @pl.when(me < owners)
    def _():
        for k in others:
            spread_copy(k).wait_send()

    for copy in placed:
        copy.wait()


def exchange(sizes, tokens, cotangent, gain_rows, keys, w1, w2):
    dp, experts, tensor = sizes
    images, count, features = tokens.shape
    units = w1.shape[1]
    slots = experts * SLOT_PER
    pair = 2 if images % 2 == 0 else 1
    chunks = images // pair
    quarter = pair * SLOT_PER
    height = 2 * quarter
    own = experts * quarter
    group = tensor * own
    spread = dp if dp <= 2 else 1
    total = spread * chunks * group
    finish = spread == dp and features % (128 * dp) == 0
    width = features // dp if finish else features
    devices = dp * experts * tensor
    lanes = features // 128
    count_tiles = slots // 8 * lanes + -(-lanes // 8)
    each = -(-count_tiles // devices)
    owners = -(-count_tiles // each)
    perms = tables(pair, experts, tensor)
    dma = pltpu.SemaphoreType.DMA
    vmem = pltpu.VMEM
    ins = dict(x_in=tokens, c_in=cotangent, gain_in=gain_rows, keys_in=keys, w1_in=w1, w2_in=w2,
               mixes_in=perms[0], unp_in=perms[1], ret_in=perms[2], sel_in=perms[3])
    outs = dict(
        stat_out=((images, count, 128), WIDE),
        s_out=((total, width), LOW), g_out=((total, width), LOW),
        h_out=((total, units), LOW), p_out=((total, units), LOW),
        left_out=((images, 4 * slots, count), LOW), right_out=((images, slots, features), LOW),
        moment_out=((images, 8, count), WIDE),
        summed_out=((owners, each * 8, 128), WIDE),
    )
    scratch = dict(
        x=vmem(tokens.shape, LOW), c=vmem(tokens.shape, LOW), normed=vmem(tokens.shape, LOW),
        gain_rows=vmem(gain_rows.shape, WIDE), gains=vmem((1, features), WIDE),
        keys=vmem(keys.shape, LOW), w1=vmem(w1.shape, LOW), w2=vmem(w2.shape, LOW),
        mixes=vmem(perms[0].shape, LOW), unp=vmem(perms[1].shape, LOW),
        turn=vmem(perms[2].shape, LOW), sel=vmem(perms[3].shape, LOW),
        stat=vmem((images, count, 128), WIDE),
        logits=vmem((images, slots, count), WIDE), disp=vmem((images, slots, count), WIDE),
        comb=vmem((images, slots, count), WIDE), slot_in=vmem((images, slots, features), WIDE),
        stack=vmem((2 * pair * slots, features), LOW), found=vmem((2 * pair * slots, features), LOW),
        blk=vmem((chunks, experts, height, features), LOW),
        rows=vmem((chunks, spread, tensor, experts, height, features), LOW),
        s_all=vmem((total, features), LOW), g_all=vmem((total, features), LOW),
        h_all=vmem((total, units), LOW), p_all=vmem((total, units), LOW),
        pre=vmem((chunks * group if spread > 1 else group, units), WIDE),
        part=vmem((chunks, 2, group, features), WIDE),
        sent=vmem((chunks, 2, max(tensor - 1, 1), own, features), LOW),
        got=vmem((chunks, 2, max(tensor - 1, 1), own, features), LOW),
        ret=vmem((chunks, experts, height, features), LOW),
        back=vmem((chunks, experts, height, features), LOW),
        left=vmem((images, 4 * slots, count), LOW), right=vmem((images, slots, features), LOW),
        moment=vmem((images, 8, count), WIDE),
        keys_sum=vmem((slots, features), WIDE), gain_sum=vmem((slots, features), WIDE),
        pack=vmem((owners if owners > devices else devices, each * 8, 128), WIDE),
        heap=vmem((devices, each * 8, 128), WIDE), total=vmem((each * 8, 128), WIDE),
        summed=vmem((devices, each * 8, 128), WIDE),
        in_sem=dma((8,)), image_sem=dma((2, images)), out_sem=dma((len(outs),)),
        zs=dma((chunks, experts)), zr=dma((chunks, experts)),
        ys=dma((chunks, tensor, experts)), yr=dma((chunks, tensor, experts)),
        xs=dma((chunks, tensor, spread)), xr=dma((chunks, tensor, spread)),
        ps=dma((chunks, 2, tensor)), pr=dma((chunks, 2, tensor)),
        bs=dma((chunks, experts)), br=dma((chunks, experts)),
        ss=dma((devices,)), sr=dma((devices,)), gs=dma((devices,)), gr=dma((devices,)),
    )
    far = pl.BlockSpec(memory_space=pltpu.HBM)
    names = list(ins) + list(outs) + list(scratch)
    values = pl.pallas_call(
        functools.partial(exchange_kernel, sizes, spread, names),
        out_shape=[jax.ShapeDtypeStruct(shape, kind) for shape, kind in outs.values()],
        in_specs=[far] * len(ins),
        out_specs=[far] * len(outs),
        scratch_shapes=list(scratch.values()),
        compiler_params=pltpu.CompilerParams(
            collective_id=0, has_side_effects=True, vmem_limit_bytes=56 * 1024 * 1024
        ),
        name="exchange",
    )(*ins.values())
    return dict(zip(outs, values)), finish


def finish_kernel(sizes, names, *refs):
    r = types.SimpleNamespace(**dict(zip(names, refs)))
    images, count, features = r.x.shape
    slots = r.keys.shape[0]
    lanes = features // 128
    products = hasattr(r, "s_in")
    fetched = {}

    def fetch(key, src, dst):
        fetched[key] = pltpu.make_async_copy(src, dst, r.in_sem.at[len(fetched)])
        fetched[key].start()

    if products:
        for key in ("s", "p", "h", "g"):
            fetch(key, getattr(r, key + "_in"), getattr(r, key))
    fetch("keys", r.keys_in, r.keys)
    fetch("gain", r.gain_in, r.gain_rows)
    fetch("moment", r.moment_in, r.moment)
    fetch("left", r.left_in, r.left)
    fetch("right", r.right_in, r.right)
    fetch("stat", r.stat_in, r.stat)
    fetch("summed", r.summed_in, r.summed)

    def image_copy(b, n):
        return pltpu.make_async_copy(
            (r.x_in, r.c_in)[n].at[b], (r.x, r.c)[n].at[b], r.image_sem.at[n, b])

    for b in range(images):
        image_copy(b, 0).start()
        image_copy(b, 1).start()

    placed = []

    def place_out(src, dst):
        copy = pltpu.make_async_copy(src, dst, r.out_sem.at[len(placed)])
        copy.start()
        placed.append(copy)

    if products:
        units = r.p.shape[1]
        fetched["s"].wait()
        r.turned[...] = r.s[...].T
        fetched["p"].wait()

        @pl.loop(0, units // TILE)
        def _(n):
            cols = pl.ds(pl.multiple_of(n * TILE, TILE), TILE)
            r.gin[:, cols] = jnp.dot(
                r.turned[...], r.p[:, cols], preferred_element_type=WIDE).astype(LOW)

        place_out(r.gin, r.gin_out)
        fetched["h"].wait()
        fetched["g"].wait()

        @pl.loop(0, units // TILE)
        def _(n):
            cols = pl.ds(pl.multiple_of(n * TILE, TILE), TILE)
            r.gout[cols, :] = contract_rows(r.h[:, cols], r.g[...]).astype(LOW)

        place_out(r.gout, r.gout_out)
    for key in ("keys", "gain", "moment", "left", "right", "stat", "summed"):
        fetched[key].wait()
    each = r.summed.shape[1] // 8
    bands = slots // 8
    for n in range(bands * lanes):
        band, lane = n // lanes, n % lanes
        r.keys_sum[band * 8:band * 8 + 8, lane * 128:lane * 128 + 128] = r.summed[
            n // each, pl.ds(n % each * 8, 8), :]
    for n in range(lanes):
        m = bands * lanes + n // 8
        row = m % each * 8 + n % 8
        r.gain_sum[n:n + 1, :] = r.summed[m // each, row:row + 1, :]
    place_out(r.keys_sum, r.keys_out)
    place_out(r.gain_sum, r.gain_out)
    r.gains[...] = jnp.concatenate([r.gain_rows[n:n + 1, :] for n in range(lanes)], axis=1)

    @pl.loop(0, images)
    def _(b):
        moment = r.moment[b].T
        average, inverse = r.stat[b, :, 0:1], r.stat[b, :, 1:2]
        r.cols[0] = jnp.broadcast_to(average, (count, 128))
        r.cols[1] = jnp.broadcast_to(inverse, (count, 128))
        r.cols[2] = jnp.broadcast_to(moment[:, 0:1], (count, 128))
        r.cols[3] = jnp.broadcast_to(-inverse * inverse * moment[:, 1:2], (count, 128))
        image_copy(b, 0).wait()
        image_copy(b, 1).wait()
        key = r.keys[...]
        r.weights[0:slots, :] = r.right[b]
        for n in range(1, 4):
            r.weights[n * slots:(n + 1) * slots, :] = key

        @pl.loop(0, lanes)
        def _(n):
            cols = pl.ds(pl.multiple_of(n * 128, 128), 128)
            grads = contract_rows(r.left[b], r.weights[:, cols]) * r.gains[:, cols]
            scaled = (r.x[b, :, cols].astype(WIDE) - r.cols[0]) * r.cols[3]
            change = r.cols[1] * (grads - r.cols[2]) + scaled
            r.out[b, :, cols] = (r.c[b, :, cols].astype(WIDE) + change).astype(LOW)

        pltpu.make_async_copy(r.out.at[b], r.tokens_out.at[b], r.image_out.at[b]).start()

    for copy in placed:
        copy.wait()
    for b in range(images):
        pltpu.make_async_copy(r.out.at[b], r.tokens_out.at[b], r.image_out.at[b]).wait()


def finish_up(sizes, tokens, cotangent, gain_rows, keys, mid, products):
    images, count, features = tokens.shape
    slots = keys.shape[0]
    dma, vmem = pltpu.SemaphoreType.DMA, pltpu.VMEM
    ins = dict(x_in=tokens, c_in=cotangent, gain_in=gain_rows, keys_in=keys,
               stat_in=mid["stat_out"], left_in=mid["left_out"], right_in=mid["right_out"],
               moment_in=mid["moment_out"], summed_in=mid["summed_out"])
    outs = dict(tokens_out=(tokens.shape, LOW), gain_out=(gain_rows.shape, WIDE),
                keys_out=(keys.shape, WIDE))
    scratch = dict(
        x=vmem(tokens.shape, LOW), c=vmem(tokens.shape, LOW), out=vmem(tokens.shape, LOW),
        gain_rows=vmem(gain_rows.shape, WIDE), gains=vmem((1, features), WIDE),
        keys=vmem(keys.shape, LOW), weights=vmem((4 * slots, features), LOW),
        cols=vmem((4, count, 128), WIDE),
        keys_sum=vmem(keys.shape, WIDE), gain_sum=vmem(gain_rows.shape, WIDE),
        in_sem=dma((16,)), image_sem=dma((2, images)), image_out=dma((images,)), out_sem=dma((4,)),
    )
    for key in ("stat", "left", "right", "moment", "summed"):
        scratch[key] = vmem(mid[key + "_out"].shape, mid[key + "_out"].dtype)
    if products:
        for key in ("s", "g", "h", "p"):
            ins[key + "_in"] = mid[key + "_out"]
            scratch[key] = vmem(mid[key + "_out"].shape, LOW)
        total, width = mid["s_out"].shape
        units = mid["p_out"].shape[1]
        scratch.update(turned=vmem((width, total), LOW), gin=vmem((width, units), LOW),
                       gout=vmem((units, width), LOW))
        outs.update(gin_out=((width, units), LOW), gout_out=((units, width), LOW))
    far = pl.BlockSpec(memory_space=pltpu.HBM)
    names = list(ins) + list(outs) + list(scratch)
    return pl.pallas_call(
        functools.partial(finish_kernel, sizes, names),
        out_shape=[jax.ShapeDtypeStruct(shape, kind) for shape, kind in outs.values()],
        in_specs=[far] * len(ins),
        out_specs=[far] * len(outs),
        scratch_shapes=list(scratch.values()),
        compiler_params=pltpu.CompilerParams(vmem_limit_bytes=56 * 1024 * 1024),
        name="finish",
    )(*ins.values())


def local(sizes, tokens, cotangent, norm_gain, slot_keys, w_in, w_out):
    dp = sizes[0]
    features = tokens.shape[2]
    gain_rows, keys = norm_gain.reshape(features // 128, 128), slot_keys.T
    mid, finish = exchange(sizes, tokens, cotangent, gain_rows, keys, w_in[0], w_out[0])
    grad_tokens, grad_gain, grad_keys, *rest = finish_up(
        sizes, tokens, cotangent, gain_rows, keys, mid, finish)
    if finish:
        first_total, second_total = rest
    else:
        slot_rows, grad_rows, hidden, grad_pre = (mid[k + "_out"] for k in ("s", "g", "h", "p"))
        if dp > 2:
            slot_rows = lax.all_to_all(slot_rows, "dp", split_axis=1, concat_axis=0, tiled=True)
            grad_rows = lax.all_to_all(grad_rows, "dp", split_axis=1, concat_axis=0, tiled=True)
            hidden = lax.all_gather(hidden, "dp", axis=0, tiled=True)
            grad_pre = lax.all_gather(grad_pre, "dp", axis=0, tiled=True)
        else:
            width = features // dp
            start = lax.axis_index("dp") * width
            slot_rows = lax.dynamic_slice_in_dim(slot_rows, start, width, axis=1)
            grad_rows = lax.dynamic_slice_in_dim(grad_rows, start, width, axis=1)
        first_total = contract_rows(slot_rows, grad_pre).astype(LOW)
        second_total = contract_rows(hidden, grad_rows).astype(LOW)
    return (
        grad_tokens, grad_gain.reshape(features), grad_keys.T,
        first_total[None], second_total[None],
    )


def solution(mesh):
    tokens = P(("dp", "expert", "tensor"), None, None)
    return jax.shard_map(
        functools.partial(local, tuple(mesh.shape[name] for name in AXES)),
        mesh=mesh,
        in_specs=(tokens, tokens, P(), P(), P("expert", None, "tensor"), P("expert", "tensor", None)),
        out_specs=(tokens, P(), P(), P("expert", "dp", "tensor"), P("expert", "tensor", "dp")),
        check_vma=False,
    )
```

time: 129 us -> 94.4 us (0.73)
  local copies, waits for them, and re-layouts: 28 us -> 0 us
  Pallas kernels: 99.1 us -> 93.6 us
    unnamed x42 -> x0, local copies, waits for them, and re-layouts: 23.4 us -> none
    pallas_call x4 -> x2, Pallas kernels: 99.1 us -> 93.6 us  [the longest x1 72.9 us: exchange(): pl.pallas_call(functools.partial(exchange_kernel, sizes, spread, names),...]
    reshape x3 -> x0, local copies, waits for them, and re-layouts: 2.37 us -> none  [the longest x1 1.01 us: reduce_all(): flat = jnp.concatenate([v.reshape(-1) for v in values])]
    slice x2 -> x0, local copies, waits for them, and re-layouts: 2.19 us -> none  [reduce_all(): results.append(summed[start:start + v.size].reshape(v.shape))]
where the time goes in v1:
time: 94.4 us; the launch traced here: 94.2 us
  Pallas kernels  93.6 us (99%)
    pallas_call x1, Pallas kernels, exchange(): pl.pallas_call(functools.partial(exchange_kernel, sizes, spread, names),...  72.9 us
    pallas_call x1, Pallas kernels, finish_up(): pl.pallas_call(functools.partial(finish_kernel, sizes, names), out_shape=...  20.6 us

profile of v1, /device:TPU:0, one launch (start us, length us, event | category | flops | bytes accessed | tf_op | source)
XLA Modules:
  0.0 94.2 jit_solution(288790247667591074)
XLA Ops:
  0.6 72.9 %exchange.1 = (f32[6,256,128]{2,1,0:T(8,128)}, bf16[384,640]{1,0:T(8,128)(2,1)}, bf16[384,640]{1,0:T(8,128)(2,1)}, bf16[384,1280]{1,0:T(8,128)(2,1)}, bf16[384,1...) custom-call(bf16[6,256,1280]{2,1,0:T(8,128)(2,1)} %refs_0_.3, ...), custom_call_target="tpu_custom_call" | custom-call | tf_op jit(solution)/shard_map/exchange/pallas_call | solution.py:509
  73.6 20.6 %finish.1 = (bf16[6,256,1280]{2,1,0:T(8,128)(2,1)}, f32[10,128]{1,0:T(8,128)}, f32[16,1280]{1,0:T(8,128)}, bf16[640,1280]{1,0:T(8,128)(2,1)}, bf16[1280,640]{1,0:T(8,128)(2,1)}) custom-call(bf16[6,256,1280]{2,1,0:T(8,128)(2,1)} %refs_0_.3, bf16[6,256,1280]{2,1,0:T(8,128)(2,1)} %refs_1_.3, f32[10,128]{1,0:T(8,128)} %bitcast.13, bf16[16,1280]{1,0:T(8,128)(2,1)} %bitcast.11, ...), custom_call_target="tpu_custom_call" | custom-call | tf_op jit(solution)/shard_map/finish/pallas_call | solution.py:660

commit v2 on v1

v2 whole, which is shorter than its diff:
```python
import functools
import types

import jax
import jax.numpy as jnp
from jax import lax
from jax.experimental import pallas as pl
from jax.experimental.pallas import tpu as pltpu
from jax.sharding import PartitionSpec as P

AXES = ("dp", "expert", "tensor")
MESH = pl.DeviceIdType.MESH
SLOT_PER = 2
EPSILON = 1e-06
GELU_A = 0.7978845608028654
GELU_B = 0.044715
TILE = 256
ROWS = 64
LOW, WIDE = jnp.bfloat16, jnp.float32
LIMIT = 40 * 1024 * 1024


def contract_rows(left, right):
    return lax.dot_general(left, right, (((0,), (0,)), ((), ())), preferred_element_type=WIDE)


def contract_cols(left, right):
    return lax.dot_general(left, right, (((1,), (1,)), ((), ())), preferred_element_type=WIDE)


def gelu_of(x):
    return 0.5 * x * (1.0 + jnp.tanh(GELU_A * (x + GELU_B * (x * x * x))))


def gelu_slope(x):
    square = x * x
    bend = jnp.tanh(GELU_A * (x + GELU_B * (square * x)))
    return 0.5 * (1.0 + bend) + 0.5 * x * (1.0 - bend * bend) * (
        GELU_A * (1.0 + 3.0 * GELU_B * square)
    )


def around(position, step, size):
    return lax.rem(position + (step + size), size)


def orders(pair, experts, tensor):
    slots, quarter = experts * SLOT_PER, pair * SLOT_PER
    height, own = 2 * quarter, experts * quarter
    group = tensor * own

    def hot(size, source):
        row = lax.broadcasted_iota(jnp.int32, (size, size), 0)
        return (source(row) == lax.broadcasted_iota(jnp.int32, (size, size), 1)).astype(LOW)

    def image_order(r):
        e, stream, u = r // height, r % height // quarter, r % quarter
        return stream * (pair * slots) + u // SLOT_PER * slots + e * SLOT_PER + u % SLOT_PER

    def stream_order(r):
        e, stream, u = r // height, r % height // quarter, r % quarter
        return stream * own + e * quarter + u

    def block_order(r):
        return r % group // quarter * height + r // group * quarter + r % quarter

    def back_order(r):
        image, stream, slot = r // (2 * slots), r % (2 * slots) // slots, r % slots
        return slot // SLOT_PER * height + stream * quarter + image * SLOT_PER + slot % SLOT_PER

    rows = experts * height
    sizes = (rows, 2 * group, rows, rows)
    sources = (image_order, block_order, stream_order, back_order)
    return [functools.partial(hot, *pair) for pair in zip(sizes, sources)]


def exchange_kernel(sizes, spread, finish, names, *refs):
    dp, experts, tensor = sizes
    r = types.SimpleNamespace(**dict(zip(names, refs)))
    d, e, t = (lax.axis_index(name) for name in AXES)
    images, count, features = r.x.shape
    slots, units = r.keys.shape[0], r.w1.shape[1]
    chunks, _, height, _ = r.blk.shape
    pair, quarter = images // chunks, height // 2
    own = experts * quarter
    group = tensor * own
    lanes = features // 128
    mine = d if spread > 1 else 0
    where = [d, e, t]

    def push(src, dst, send, recv, axis, place):
        target = {"dp": d, "expert": e, "tensor": t}
        target[axis] = place
        return pltpu.make_async_remote_copy(
            src_ref=src, dst_ref=dst, send_sem=send, recv_sem=recv,
            device_id=tuple(target[name] for name in AXES), device_id_type=MESH,
        )

    def columns(tile, extent=features):
        return [slice(n, n + tile) for n in range(0, extent, tile)]

    started = []

    def launch(copy):
        copy.start()
        started.append(copy)

    offsets = [(a, b, c) for a in range(dp) for b in range(experts) for c in range(tensor)]
    targets = [tuple(around(w, k, s) for w, k, s in zip(where, step, sizes)) for step in offsets]
    sources = [tuple(around(w, -k, s) for w, k, s in zip(where, step, sizes)) for step in offsets]
    others = range(1, len(offsets))
    rank = lambda p: (p[0] * experts + p[1]) * tensor + p[2]

    fetched = []

    def fetch(src, dst):
        copy = pltpu.make_async_copy(src, dst, r.in_sem.at[len(fetched)])
        copy.start()
        fetched.append(copy)
        return copy

    def image_copy(b, n):
        return pltpu.make_async_copy(
            (r.x_in, r.c_in)[n].at[b], (r.x, r.c)[n].at[b], r.image_sem.at[n, b])

    small = [fetch(r.gain_in, r.gain_rows), fetch(r.keys_in, r.keys)]
    for b in range(pair):
        image_copy(b, 0).start()
        image_copy(b, 1).start()
    barrier = pltpu.get_barrier_semaphore()
    for k in others:
        pl.semaphore_signal(barrier, inc=1, device_id=targets[k], device_id_type=MESH)
    for b in range(pair, images):
        image_copy(b, 0).start()
        image_copy(b, 1).start()
    w1_copy, w2_copy = fetch(r.w1_in, r.w1), fetch(r.w2_in, r.w2)
    image_order, block_order, stream_order, back_order = orders(pair, experts, tensor)
    for copy in small:
        copy.wait()
    r.gains[...] = jnp.concatenate([r.gain_rows[n:n + 1, :] for n in range(lanes)], axis=1)
    r.keys_sum[...] = jnp.zeros_like(r.keys_sum)
    r.gain_sum[...] = jnp.zeros_like(r.gain_sum)

    def normalise(b):
        blocks = [slice(n, n + ROWS) for n in range(0, count, ROWS)]
        for rows in blocks:
            average = jnp.mean(r.x[b, rows, :].astype(WIDE), axis=-1, keepdims=True)
            r.average[b, rows, :] = jnp.broadcast_to(average, (ROWS, 128))
        for rows in blocks:
            average = r.average[b, rows, :]
            square = jnp.zeros((ROWS, 128), WIDE)
            for lane in columns(128):
                centred = r.x[b, rows, lane].astype(WIDE) - average
                square = square + centred * centred
            spread_of = jnp.sum(square, axis=-1, keepdims=True) * (1.0 / features)
            r.inverse[b, rows, :] = jnp.broadcast_to(lax.rsqrt(spread_of + EPSILON), (ROWS, 128))
        for rows in blocks:
            average, inverse = r.average[b, rows, :], r.inverse[b, rows, :]
            for lane in columns(128):
                centred = r.x[b, rows, lane].astype(WIDE) - average
                r.normed[b, rows, lane] = (centred * inverse * r.gains[:, lane]).astype(LOW)

    def mix_image(b, slab):
        logits = contract_cols(r.keys[...], r.normed[b])
        over_tokens = jnp.exp(logits - jnp.max(logits, axis=1, keepdims=True))
        over_tokens = over_tokens / jnp.sum(over_tokens, axis=1, keepdims=True)
        over_slots = jnp.exp(logits - jnp.max(logits, axis=0, keepdims=True))
        over_slots = over_slots / jnp.sum(over_slots, axis=0, keepdims=True)
        r.logits[b] = logits
        r.disp[b] = over_tokens
        r.comb[b] = over_slots
        taken = jnp.dot(over_tokens.astype(LOW), r.normed[b], preferred_element_type=WIDE)
        given = jnp.dot(over_slots.astype(LOW), r.c[b], preferred_element_type=WIDE)
        r.slot_in[b] = taken
        r.stack[slab * slots:(slab + 1) * slots, :] = taken.astype(LOW)
        r.stack[(pair + slab) * slots:(pair + slab + 1) * slots, :] = given.astype(LOW)

    def mix(c):
        if c == 0:
            r.mixes[...] = image_order()
        for slab in range(pair):
            image_copy(c * pair + slab, 0).wait()
            image_copy(c * pair + slab, 1).wait()
        for slab in range(pair):
            normalise(c * pair + slab)
        for slab in range(pair):
            mix_image(c * pair + slab, slab)
        moved = jnp.dot(r.mixes[...], r.stack[...], preferred_element_type=WIDE)
        for n in range(experts):
            r.blk[c, n] = moved[n * height:(n + 1) * height].astype(LOW)

    near = sorted(range(1, experts), key=lambda k: -min(k, experts - k))
    arrive = {}

    def scatter(c):
        for k in near:
            to = around(e, k, experts)
            arrive[c, k] = push(r.blk.at[c, to], r.rows.at[c, mine, t, e],
                                r.zs.at[c, k], r.zr.at[c, k], "expert", to)
            launch(arrive[c, k])
        share_rows(c, r.blk.at[c, e], 0)
        r.rows[c, mine, t, e] = r.blk[c, e]

    def share_rows(c, src, k):
        slot = r.rows.at[c, mine, t, around(e, -k, experts)]
        for j in range(1, tensor):
            launch(push(src, slot, r.ys.at[c, j, k], r.yr.at[c, j, k], "tensor", around(t, j, tensor)))

    def share_slab(c, j):
        for i in range(1, spread):
            slab = r.rows.at[c, mine, around(t, -j, tensor)]
            launch(push(slab, slab, r.xs.at[c, j, i], r.xr.at[c, j, i], "dp", around(d, i, dp)))

    def forward_rows(c):
        for k in near:
            arrive[c, k].wait_recv()
            share_rows(c, r.rows.at[c, mine, t, around(e, -k, experts)], k)
        share_slab(c, 0)

    def gather_rows(c):
        for j in range(1, tensor):
            for k in [0] + near:
                slot = r.rows.at[c, mine, around(t, -j, tensor), around(e, -k, experts)]
                push(slot, slot, r.ys.at[c, j, k], r.yr.at[c, j, k],
                     "tensor", around(t, j, tensor)).wait_recv()
            share_slab(c, j)

    def unpack(c, place, base):
        block = r.rows[c, place].reshape(2 * group, features)
        both = jnp.dot(r.unp[...], block, preferred_element_type=WIDE)
        r.s_all[base:base + group, :] = both[0:group].astype(LOW)
        r.g_all[base:base + group, :] = both[group:].astype(LOW)

    def transpose(weight, turned):
        row = lax.broadcasted_iota(jnp.int32, (TILE, TILE), 0)
        eye = (row == lax.broadcasted_iota(jnp.int32, (TILE, TILE), 1)).astype(LOW)

        @pl.loop(0, weight.shape[0] // TILE)
        def _(n):
            rows = pl.ds(pl.multiple_of(n * TILE, TILE), TILE)
            for cols in columns(TILE, weight.shape[1]):
                turned[cols, rows] = contract_cols(eye, weight[rows, cols]).astype(LOW)

    def forward(base, size):
        for cols in columns(TILE, units):
            x = jnp.dot(r.s_all[base:base + size, :], r.w1[:, cols], preferred_element_type=WIDE)
            r.pre[0:size, cols] = x
            r.h_all[base:base + size, cols] = gelu_of(x).astype(LOW)

    def backward(base, size):
        for cols in columns(TILE, units):
            x = jnp.dot(r.g_all[base:base + size, :], r.w2_turned[:, cols], preferred_element_type=WIDE)
            r.p_all[base:base + size, cols] = (x * gelu_slope(r.pre[0:size, cols])).astype(LOW)

    def project(c, base):
        for cols in columns(TILE):
            r.part[c, 0, :, cols] = jnp.dot(
                r.h_all[base:base + group, :], r.w2[:, cols], preferred_element_type=WIDE)
        share_part(c, 0)

    def project_back(c, base):
        for cols in columns(TILE):
            r.part[c, 1, :, cols] = jnp.dot(
                r.p_all[base:base + group, :], r.w1_turned[:, cols], preferred_element_type=WIDE)
        share_part(c, 1)

    def part_copy(c, which, j):
        return push(r.sent.at[c, which, j - 1], r.got.at[c, which, j - 1],
                    r.ps.at[c, which, j], r.pr.at[c, which, j], "tensor", around(t, j, tensor))

    def share_part(c, which):
        for j in range(1, tensor):
            to = around(t, j, tensor)
            r.sent[c, which, j - 1] = r.part[c, which, pl.ds(pl.multiple_of(to * own, 8), own), :].astype(LOW)
            launch(part_copy(c, which, j))

    def give_back(c):
        totals = []
        for which in range(2):
            total = r.part[c, which, pl.ds(pl.multiple_of(t * own, 8), own), :]
            for j in range(1, tensor):
                part_copy(c, which, j).wait_recv()
                total = total + r.got[c, which, j - 1].astype(WIDE)
            totals.append(total.astype(LOW))
        moved = jnp.dot(r.turn[...], jnp.concatenate(totals, axis=0), preferred_element_type=WIDE)
        for n in range(experts):
            r.ret[c, n] = moved[n * height:(n + 1) * height].astype(LOW)
        for k in near:
            to = around(e, k, experts)
            arrive["back", c, k] = push(r.ret.at[c, to], r.back.at[c, e],
                                        r.bs.at[c, k], r.br.at[c, k], "expert", to)
            launch(arrive["back", c, k])
        r.back[c, e] = r.ret[c, e]

    def image_gradients(b, slab):
        start = slab * 2 * slots
        returned = r.found[start:start + slots, :]
        slot_grad = r.found[start + slots:start + 2 * slots, :]
        grad_dispatch = contract_cols(slot_grad, r.normed[b])
        grad_combine = contract_cols(returned, r.c[b])
        dispatch, combine = r.disp[b], r.comb[b]
        logit = dispatch * (
            grad_dispatch - jnp.sum(dispatch * grad_dispatch, axis=1, keepdims=True)
        ) + combine * (grad_combine - jnp.sum(combine * grad_combine, axis=0, keepdims=True))
        first = logit.astype(LOW)
        rest = logit - first.astype(WIDE)
        second = rest.astype(LOW)
        third = (rest - second.astype(WIDE)).astype(LOW)
        low = dispatch.astype(LOW)
        split = jnp.concatenate([first, second, third], axis=0)
        r.left[b, 0:slots, :] = low
        r.left[b, slots:4 * slots, :] = split
        r.right[b] = slot_grad
        parts = jnp.dot(split, r.normed[b], preferred_element_type=WIDE)
        r.keys_sum[...] += parts[0:slots] + parts[slots:2 * slots] + parts[2 * slots:3 * slots]
        wide = slot_grad.astype(WIDE)
        r.gain_sum[...] += wide * r.slot_in[b]
        low = low.astype(WIDE)
        gains = r.gains[...]
        from_slots = jnp.sum(wide * gains, axis=1, keepdims=True)
        from_keys = jnp.sum(r.keys[...].astype(WIDE) * gains, axis=1, keepdims=True)
        first_mean = jnp.sum(low * from_slots + logit * from_keys, axis=0, keepdims=True)
        second_mean = jnp.sum(low * grad_dispatch + logit * r.logits[b], axis=0, keepdims=True)
        row = lax.broadcasted_iota(jnp.int32, (8, count), 0)
        r.moment[b] = jnp.where(row == 0, first_mean, second_mean) * (1.0 / features)

    def take_back(c):
        with jax.named_scope(f"waitback{c}"):
            for k in near:
                arrive["back", c, k].wait_recv()
        block = r.back[c].reshape(experts * height, features)
        r.found[...] = jnp.dot(r.sel[...], block, preferred_element_type=WIDE).astype(LOW)

        for slab in range(pair):
            image_gradients(c * pair + slab, slab)

    placed = []

    def place_out(src, dst):
        copy = pltpu.make_async_copy(src, dst, r.out_sem.at[len(placed)])
        copy.start()
        placed.append(copy)

    def finish_image(b):
        moment = r.moment[b].T
        average, inverse = r.average[b], r.inverse[b]
        first = jnp.broadcast_to(moment[:, 0:1], (count, 128))
        second = -inverse * inverse * moment[:, 1:2]
        r.cols[0] = first
        r.cols[1] = second
        left = r.left[b].T
        key = r.keys[...]
        for cols in columns(TILE):
            right = jnp.concatenate([r.right[b, :, cols]] + [key[:, cols]] * 3, axis=0)
            grads = jnp.dot(left, right, preferred_element_type=WIDE) * r.gains[:, cols]
            for n in range(0, TILE, 128):
                lane = slice(cols.start + n, cols.start + n + 128)
                scaled = (r.x[b, :, lane].astype(WIDE) - r.average[b]) * r.cols[1]
                change = r.inverse[b] * (grads[:, n:n + 128] - r.cols[0]) + scaled
                r.x[b, :, lane] = (r.c[b, :, lane].astype(WIDE) + change).astype(LOW)

    full = chunks * group

    def other_rows(i):
        other = around(d, -i, dp)
        for c in range(chunks):
            for j in range(tensor):
                slab = r.rows.at[c, other, around(t, -j, tensor)]
                push(slab, slab, r.xs.at[c, j, i], r.xr.at[c, j, i], "dp", around(d, i, dp)).wait_recv()
            unpack(c, other, i * full + c * group)

    scope = jax.named_scope
    steps = []

    def step(name, action):
        with scope(name):
            action()

    def turn_weight(copy, weight, turned):
        copy.wait()
        transpose(weight, turned)

    last = chunks - 1
    for c in range(chunks):
        step(f"mix{c}", lambda: mix(c))
        if c == 0:
            step("barrier", lambda: pl.semaphore_wait(barrier, len(others)))
        step(f"scatter{c}", lambda: scatter(c))
    step("fwdrows0", lambda: forward_rows(0))
    r.unp[...], r.turn[...], r.sel[...] = block_order(), stream_order(), back_order()
    step("weights2", lambda: turn_weight(w2_copy, r.w2, r.w2_turned))
    if chunks > 1:
        step("fwdrows1", lambda: forward_rows(1))
    step("weights1", lambda: turn_weight(w1_copy, r.w1, r.w1_turned))
    for c in range(chunks):
        base = c * group
        step(f"gather{c}", lambda: gather_rows(c))
        step(f"unpack{c}", lambda: unpack(c, mine, base))
        step(f"forward{c}", lambda: forward(base, group))
        step(f"project{c}", lambda: project(c, base))
        if c + 2 < chunks:
            step(f"fwdrows{c + 2}", lambda: forward_rows(c + 2))
        step(f"backward{c}", lambda: backward(base, group))
        step(f"projback{c}", lambda: project_back(c, base))
        if c > 0:
            step(f"giveback{c - 1}", lambda: give_back(c - 1))
    if chunks > 2:
        step("takeback0", lambda: take_back(0))
    for i in range(1, spread):
        step("otherrows", lambda: other_rows(i))
        step("otherfwd", lambda: forward(i * full, full))
    step(f"giveback{last}", lambda: give_back(last))
    for c in range(1 if chunks > 2 else 0, last):
        step(f"takeback{c}", lambda: take_back(c))
    for i in range(1, spread):
        step("otherbwd", lambda: backward(i * full, full))
    if finish:
        width = r.gin.shape[0]
        mine_cols = pl.ds(pl.multiple_of(d * width, 128), width)

        def product_in():
            r.turned[...] = r.s_all[:, mine_cols].T

            @pl.loop(0, units // TILE)
            def _(n):
                cols = pl.ds(pl.multiple_of(n * TILE, TILE), TILE)
                r.gin[:, cols] = jnp.dot(
                    r.turned[...], r.p_all[:, cols], preferred_element_type=WIDE).astype(LOW)

        def product_out():
            @pl.loop(0, units // TILE)
            def _(n):
                cols = pl.ds(pl.multiple_of(n * TILE, TILE), TILE)
                r.gout[cols, :] = contract_rows(r.h_all[:, cols], r.g_all[:, mine_cols]).astype(LOW)

        step("productin", product_in)
    else:
        place_out(r.s_all, r.s_out)
        place_out(r.g_all, r.g_out)
        place_out(r.h_all, r.h_out)
        place_out(r.p_all, r.p_out)
    step(f"takeback{last}", lambda: take_back(last))

    each = r.pack.shape[1] // 8
    bands = slots // 8
    count_tiles = bands * lanes + -(-lanes // 8)
    owners = -(-count_tiles // each)
    me = rank(where)
    gain = jnp.sum(r.gain_sum[...] + r.keys[...].astype(WIDE) * r.keys_sum[...], axis=0, keepdims=True)
    gain = gain / r.gains[...]
    for n in range(bands * lanes):
        band, lane = n // lanes, n % lanes
        r.pack[n // each, pl.ds(n % each * 8, 8), :] = r.keys_sum[
            band * 8:band * 8 + 8, lane * 128:lane * 128 + 128]
    for n in range(-(-lanes // 8) * 8):
        m = bands * lanes + n // 8
        row = m % each * 8 + n % 8
        piece = gain[:, n * 128:n * 128 + 128] if n < lanes else jnp.zeros((1, 128), WIDE)
        r.pack[m // each, row:row + 1, :] = piece

    def reduce_copy(k):
        return pltpu.make_async_remote_copy(
            src_ref=r.pack.at[rank(targets[k])], dst_ref=r.heap.at[k], send_sem=r.ss.at[k],
            recv_sem=r.sr.at[k], device_id=targets[k], device_id_type=MESH)

    def spread_copy(k):
        return pltpu.make_async_remote_copy(
            src_ref=r.total, dst_ref=r.summed.at[me], send_sem=r.gs.at[k],
            recv_sem=r.gr.at[k], device_id=targets[k], device_id_type=MESH)

    def gated(test, action):
        pl.when(test)(action)

    for k in others:
        gated(rank(targets[k]) < owners, lambda k=k: reduce_copy(k).start())

    def finish_images():
        @pl.loop(0, images)
        def _(b):
            finish_image(b)

    step("elem", finish_images)

    def reduce_own():
        @pl.when(me < owners)
        def _():
            r.heap[0] = r.pack[me]
            for k in others:
                reduce_copy(k).wait_recv()
            r.total[...] = jnp.sum(r.heap[...], axis=0)
            for k in others:
                spread_copy(k).start()
            r.summed[me] = r.total[...]

    step("reduceown", reduce_own)
    if finish:
        step("productout", product_out)

    def drain():
        for copy in started:
            copy.wait_send()
        for k in others:
            gated(rank(targets[k]) < owners, lambda k=k: reduce_copy(k).wait_send())

    step("drain", drain)

    def collect():
        for k in others:
            gated(rank(sources[k]) < owners, lambda k=k: spread_copy(k).wait_recv())
        for n in range(bands * lanes):
            band, lane = n // lanes, n % lanes
            r.keys_out[band * 8:band * 8 + 8, lane * 128:lane * 128 + 128] = r.summed[
                n // each, n % each * 8:n % each * 8 + 8, :]
        for n in range(lanes):
            m = bands * lanes + n // 8
            row = m % each * 8 + n % 8
            r.gain_out[n:n + 1, :] = r.summed[m // each, row:row + 1, :]

        @pl.when(me < owners)
        def _():
            for k in others:
                spread_copy(k).wait_send()

        for copy in placed:
            copy.wait()

    step("collect", collect)


def exchange(sizes, tokens, cotangent, gain_rows, keys, w1, w2):
    dp, experts, tensor = sizes
    images, count, features = tokens.shape
    units = w1.shape[1]
    slots = experts * SLOT_PER
    pair = 2 if images % 2 == 0 else 1
    chunks = images // pair
    quarter = pair * SLOT_PER
    height = 2 * quarter
    own = experts * quarter
    group = tensor * own
    spread = dp if dp <= 2 else 1
    total = spread * chunks * group
    finish = spread == dp and features % (128 * dp) == 0
    devices = dp * experts * tensor
    lanes = features // 128
    count_tiles = slots // 8 * lanes + -(-lanes // 8)
    each = -(-count_tiles // devices)
    dma = pltpu.SemaphoreType.DMA
    vmem = pltpu.VMEM
    ins = dict(x_in=tokens, c_in=cotangent, gain_in=gain_rows, keys_in=keys, w1_in=w1, w2_in=w2)
    outs = dict(x=(tokens.shape, LOW), gain_out=(gain_rows.shape, WIDE), keys_out=(keys.shape, WIDE))
    if finish:
        outs.update(gin=((features // dp, units), LOW), gout=((units, features // dp), LOW))
    held = len(outs)
    if not finish:
        outs.update(s_out=((total, features), LOW), g_out=((total, features), LOW),
                    h_out=((total, units), LOW), p_out=((total, units), LOW))
    rows = experts * height
    scratch = dict(
        c=vmem(tokens.shape, LOW), normed=vmem(tokens.shape, LOW),
        gain_rows=vmem(gain_rows.shape, WIDE), gains=vmem((1, features), WIDE),
        keys=vmem(keys.shape, LOW), w1=vmem(w1.shape, LOW), w2=vmem(w2.shape, LOW),
        mixes=vmem((rows, rows), LOW), unp=vmem((2 * group, 2 * group), LOW),
        turn=vmem((rows, rows), LOW), sel=vmem((rows, rows), LOW),
        average=vmem((images, count, 128), WIDE), inverse=vmem((images, count, 128), WIDE),
        cols=vmem((2, count, 128), WIDE),
        w1_turned=vmem(w1.shape[::-1], LOW), w2_turned=vmem(w2.shape[::-1], LOW),
        logits=vmem((images, slots, count), WIDE), disp=vmem((images, slots, count), WIDE),
        comb=vmem((images, slots, count), WIDE), slot_in=vmem((images, slots, features), WIDE),
        stack=vmem((2 * pair * slots, features), LOW), found=vmem((2 * pair * slots, features), LOW),
        blk=vmem((chunks, experts, height, features), LOW),
        rows=vmem((chunks, spread, tensor, experts, height, features), LOW),
        s_all=vmem((total, features), LOW), g_all=vmem((total, features), LOW),
        h_all=vmem((total, units), LOW), p_all=vmem((total, units), LOW),
        pre=vmem((chunks * group if spread > 1 else group, units), WIDE),
        part=vmem((chunks, 2, group, features), WIDE),
        sent=vmem((chunks, 2, max(tensor - 1, 1), own, features), LOW),
        got=vmem((chunks, 2, max(tensor - 1, 1), own, features), LOW),
        ret=vmem((chunks, experts, height, features), LOW),
        back=vmem((chunks, experts, height, features), LOW),
        left=vmem((images, 4 * slots, count), LOW), right=vmem((images, slots, features), LOW),
        moment=vmem((images, 8, count), WIDE),
        keys_sum=vmem((slots, features), WIDE), gain_sum=vmem((slots, features), WIDE),
        pack=vmem((devices, each * 8, 128), WIDE),
        heap=vmem((devices, each * 8, 128), WIDE), total=vmem((each * 8, 128), WIDE),
        summed=vmem((devices, each * 8, 128), WIDE),
        in_sem=dma((8,)), image_sem=dma((2, images)), out_sem=dma((4,)),
        zs=dma((chunks, experts)), zr=dma((chunks, experts)),
        ys=dma((chunks, tensor, experts)), yr=dma((chunks, tensor, experts)),
        xs=dma((chunks, tensor, spread)), xr=dma((chunks, tensor, spread)),
        ps=dma((chunks, 2, tensor)), pr=dma((chunks, 2, tensor)),
        bs=dma((chunks, experts)), br=dma((chunks, experts)),
        ss=dma((devices,)), sr=dma((devices,)), gs=dma((devices,)), gr=dma((devices,)),
    )
    if finish:
        scratch.update(turned=vmem((features // dp, total), LOW))
    far, near = pl.BlockSpec(memory_space=pltpu.HBM), pl.BlockSpec(memory_space=vmem)
    names = list(ins) + list(outs) + list(scratch)
    values = pl.pallas_call(
        functools.partial(exchange_kernel, sizes, spread, finish, names),
        out_shape=[jax.ShapeDtypeStruct(shape, kind) for shape, kind in outs.values()],
        in_specs=[far] * len(ins),
        out_specs=[near] * held + [far] * (len(outs) - held),
        scratch_shapes=list(scratch.values()),
        compiler_params=pltpu.CompilerParams(
            collective_id=0, has_side_effects=True, vmem_limit_bytes=LIMIT if finish else LIMIT + LIMIT // 4
        ),
        name="exchange",
    )(*[pltpu.with_memory_space_constraint(v, pltpu.HBM) for v in ins.values()])
    return values[:held], values[held:]


def store_kernel(count, *refs):
    copies = [
        pltpu.make_async_copy(refs[n], refs[count + n], refs[-1].at[n]) for n in range(count)
    ]
    for copy in copies:
        copy.start()
    for copy in copies:
        copy.wait()


def store(values):
    count = len(values)
    return pl.pallas_call(
        functools.partial(store_kernel, count),
        out_shape=[jax.ShapeDtypeStruct(v.shape, v.dtype) for v in values],
        in_specs=[pl.BlockSpec(memory_space=pltpu.VMEM)] * count,
        out_specs=[pl.BlockSpec(memory_space=pltpu.HBM)] * count,
        scratch_shapes=[pltpu.SemaphoreType.DMA((count,))],
        compiler_params=pltpu.CompilerParams(vmem_limit_bytes=12 * 1024 * 1024),
        name="store",
    )(*values)


def local(sizes, tokens, cotangent, norm_gain, slot_keys, w_in, w_out):
    dp = sizes[0]
    features = tokens.shape[2]
    gain_rows, keys = norm_gain.reshape(features // 128, 128), slot_keys.T
    held, rows = exchange(sizes, tokens, cotangent, gain_rows, keys, w_in[0], w_out[0])
    grad_tokens, grad_gain, grad_keys, *rest = store(held)
    if rest:
        first_total, second_total = rest
    else:
        slot_rows, grad_rows, hidden, grad_pre = rows
        if dp > 2:
            slot_rows = lax.all_to_all(slot_rows, "dp", split_axis=1, concat_axis=0, tiled=True)
            grad_rows = lax.all_to_all(grad_rows, "dp", split_axis=1, concat_axis=0, tiled=True)
            hidden = lax.all_gather(hidden, "dp", axis=0, tiled=True)
            grad_pre = lax.all_gather(grad_pre, "dp", axis=0, tiled=True)
        else:
            width = features // dp
            start = lax.axis_index("dp") * width
            slot_rows = lax.dynamic_slice_in_dim(slot_rows, start, width, axis=1)
            grad_rows = lax.dynamic_slice_in_dim(grad_rows, start, width, axis=1)
        first_total = contract_rows(slot_rows, grad_pre).astype(LOW)
        second_total = contract_rows(hidden, grad_rows).astype(LOW)
    return (
        grad_tokens, grad_gain.reshape(features), grad_keys.T,
        first_total[None], second_total[None],
    )


def solution(mesh):
    tokens = P(("dp", "expert", "tensor"), None, None)
    return jax.shard_map(
        functools.partial(local, tuple(mesh.shape[name] for name in AXES)),
        mesh=mesh,
        in_specs=(tokens, tokens, P(), P(), P("expert", None, "tensor"), P("expert", "tensor", None)),
        out_specs=(tokens, P(), P(), P("expert", "dp", "tensor"), P("expert", "tensor", "dp")),
        check_vma=False,
    )
```

time: 94.4 us -> 62.3 us (0.66)
  Pallas kernels: 93.6 us -> 61.4 us
    pallas_call x2, Pallas kernels: 93.6 us -> 61.4 us  [the longest x1 58.3 us: exchange(): pl.pallas_call(functools.partial(exchange_kernel, sizes, spread, finish,...]
where the time goes in v2:
time: 62.3 us; the launch traced here: 62.2 us
  Pallas kernels  61.4 us (99%)
  between operations  0.8 us (1%)
    pallas_call x1, Pallas kernels, exchange(): pl.pallas_call(functools.partial(exchange_kernel, sizes, spread, finish,...  58.3 us
    pallas_call x1, Pallas kernels, store(): pl.pallas_call(functools.partial(store_kernel, count), out_shape=[jax.Sha...  3.08 us

profile of v2, /device:TPU:0, one launch (start us, length us, event | category | flops | bytes accessed | tf_op | source)
XLA Modules:
  0.0 62.2 jit_solution(17140415964755751530)
XLA Ops:
  0.6 58.3 %exchange.1 = (bf16[6,256,1280]{2,1,0:T(8,128)(2,1)S(1)}, f32[10,128]{1,0:T(8,128)S(1)}, f32[16,1280]{1,0:T(8,128)S(1)}, bf16[640,1280]{1,0:T(8,128)(2,1)S(1)}, bf16[1280,640]{1,0:T(8,128)(2,1)S(1)}) custom-call(bf16[6,256,1280]{2,1,0:T(8,128)(2,1)} %refs_0_.1, bf16[6,256,1280]{2,1,0:T(8,128)(2,1)} %refs_1_.1, f32[10,128]{1,0:T(8,128)} %bitcast.11, ...), custom_call_target="tpu_custom_call" | custom-call | tf_op jit(solution)/shard_map/exchange/pallas_call | solution.py:599
  58.9 3.1 %store.1 = (bf16[6,256,1280]{2,1,0:T(8,128)(2,1)}, f32[10,128]{1,0:T(8,128)}, f32[16,1280]{1,0:T(8,128)}, bf16[640,1280]{1,0:T(8,128)(2,1)}, bf16[1280,640]{1,0:T(8,128)(2,1)}) custom-call(bf16[6,256,1280]{2,1,0:T(8,128)(2,1)S(1)} %get-tuple-element.15.refs_0_, f32[10,128]{1,0:T(8,128)S(1)} %get-tuple-element.16.refs_1_, ...), custom_call_target="tpu_custom_call" | custom-call | tf_op jit(solution)/shard_map/store/pallas_call | solution.py:625

commit v3 on v2

--- a/solution.py
+++ b/solution.py
@@ -99,11 +99,11 @@
     def columns(tile, extent=features):
         return [slice(n, n + tile) for n in range(0, extent, tile)]
 
-    started = []
+    sent, returned = [], {}
 
     def launch(copy):
         copy.start()
-        started.append(copy)
+        sent.append(copy)
 
     offsets = [(a, b, c) for a in range(dp) for b in range(experts) for c in range(tensor)]
     targets = [tuple(around(w, k, s) for w, k, s in zip(where, step, sizes)) for step in offsets]
@@ -135,9 +135,6 @@
         image_copy(b, 1).start()
     w1_copy, w2_copy = fetch(r.w1_in, r.w1), fetch(r.w2_in, r.w2)
     image_order, block_order, stream_order, back_order = orders(pair, experts, tensor)
-    for copy in small:
-        copy.wait()
-    r.gains[...] = jnp.concatenate([r.gain_rows[n:n + 1, :] for n in range(lanes)], axis=1)
     r.keys_sum[...] = jnp.zeros_like(r.keys_sum)
     r.gain_sum[...] = jnp.zeros_like(r.gain_sum)
 
@@ -175,54 +172,62 @@
         r.stack[slab * slots:(slab + 1) * slots, :] = taken.astype(LOW)
         r.stack[(pair + slab) * slots:(pair + slab + 1) * slots, :] = given.astype(LOW)
 
-    def mix(c):
-        if c == 0:
-            r.mixes[...] = image_order()
-        for slab in range(pair):
-            image_copy(c * pair + slab, 0).wait()
-            image_copy(c * pair + slab, 1).wait()
-        for slab in range(pair):
-            normalise(c * pair + slab)
-        for slab in range(pair):
-            mix_image(c * pair + slab, slab)
+    def pack_rows(c):
         moved = jnp.dot(r.mixes[...], r.stack[...], preferred_element_type=WIDE)
         for n in range(experts):
             r.blk[c, n] = moved[n * height:(n + 1) * height].astype(LOW)
 
-    near = sorted(range(1, experts), key=lambda k: -min(k, experts - k))
+    def partner(k):
+        place = e
+        for bit in (1 << n for n in range(k.bit_length()) if k >> n & 1):
+            place = place + bit * (1 - 2 * lax.rem(lax.div(e, bit), 2))
+        return place
+
+    near = list(range(1, experts))
+    if experts & (experts - 1) == 0:
+        goes = comes = [partner(k) for k in range(experts)]
+    else:
+        goes = [around(e, k, experts) for k in range(experts)]
+        comes = [around(e, -k, experts) for k in range(experts)]
     arrive = {}
 
     def scatter(c):
+        share_rows(c, r.blk.at[c, e], 0)
         for k in near:
-            to = around(e, k, experts)
-            arrive[c, k] = push(r.blk.at[c, to], r.rows.at[c, mine, t, e],
-                                r.zs.at[c, k], r.zr.at[c, k], "expert", to)
-            launch(arrive[c, k])
-        share_rows(c, r.blk.at[c, e], 0)
+            arrive[c, k] = push(r.blk.at[c, goes[k]], r.rows.at[c, mine, t, e],
+                                r.zs.at[c], r.zr.at[c, k], "expert", goes[k])
+            arrive[c, k].start()
+        most = r.rows.at[c, mine, t, pl.ds(0, experts - 1)]
+        sent.append(push(most, most, r.zs.at[c], r.zr.at[c, 1], "expert", goes[1]))
         r.rows[c, mine, t, e] = r.blk[c, e]
 
     def share_rows(c, src, k):
-        slot = r.rows.at[c, mine, t, around(e, -k, experts)]
+        slot = r.rows.at[c, mine, t, comes[k]]
         for j in range(1, tensor):
-            launch(push(src, slot, r.ys.at[c, j, k], r.yr.at[c, j, k], "tensor", around(t, j, tensor)))
+            push(src, slot, r.ys.at[c, j - 1], r.yr.at[c, j - 1], "tensor", around(t, j, tensor)).start()
 
     def share_slab(c, j):
         for i in range(1, spread):
             slab = r.rows.at[c, mine, around(t, -j, tensor)]
-            launch(push(slab, slab, r.xs.at[c, j, i], r.xr.at[c, j, i], "dp", around(d, i, dp)))
-
-    def forward_rows(c):
-        for k in near:
+            launch(push(slab, slab, r.xs.at[c, j, i - 1], r.xr.at[c, j, i - 1], "dp", around(d, i, dp)))
+
+    waiting = {}
+
+    def forward_rows(c, upto=experts):
+        ready = [k for k in waiting.setdefault(c, list(near)) if k < upto]
+        for k in ready:
+            waiting[c].remove(k)
             arrive[c, k].wait_recv()
-            share_rows(c, r.rows.at[c, mine, t, around(e, -k, experts)], k)
-        share_slab(c, 0)
+            share_rows(c, r.rows.at[c, mine, t, comes[k]], k)
+        if ready and not waiting[c]:
+            share_slab(c, 0)
 
     def gather_rows(c):
         for j in range(1, tensor):
-            for k in [0] + near:
-                slot = r.rows.at[c, mine, around(t, -j, tensor), around(e, -k, experts)]
-                push(slot, slot, r.ys.at[c, j, k], r.yr.at[c, j, k],
-                     "tensor", around(t, j, tensor)).wait_recv()
+            slab = r.rows.at[c, mine, around(t, -j, tensor)]
+            whole = push(slab, slab, r.ys.at[c, j - 1], r.yr.at[c, j - 1], "tensor", around(t, j, tensor))
+            whole.wait_recv()
+            sent.append(whole)
             share_slab(c, j)
 
     def unpack(c, place, base):
@@ -266,7 +271,7 @@
 
     def part_copy(c, which, j):
         return push(r.sent.at[c, which, j - 1], r.got.at[c, which, j - 1],
-                    r.ps.at[c, which, j], r.pr.at[c, which, j], "tensor", around(t, j, tensor))
+                    r.ps.at[c, which, j - 1], r.pr.at[c, which, j - 1], "tensor", around(t, j, tensor))
 
     def share_part(c, which):
         for j in range(1, tensor):
@@ -285,11 +290,11 @@
         moved = jnp.dot(r.turn[...], jnp.concatenate(totals, axis=0), preferred_element_type=WIDE)
         for n in range(experts):
             r.ret[c, n] = moved[n * height:(n + 1) * height].astype(LOW)
-        for k in near:
-            to = around(e, k, experts)
-            arrive["back", c, k] = push(r.ret.at[c, to], r.back.at[c, e],
-                                        r.bs.at[c, k], r.br.at[c, k], "expert", to)
-            launch(arrive["back", c, k])
+        for k in reversed(near):
+            push(r.ret.at[c, goes[k]], r.back.at[c, e], r.bs.at[c], r.br.at[c], "expert", goes[k]).start()
+        most = r.back.at[c, pl.ds(0, experts - 1)]
+        returned[c] = push(most, most, r.bs.at[c], r.br.at[c], "expert", goes[1])
+        sent.append(returned[c])
         r.back[c, e] = r.ret[c, e]
 
     def image_gradients(b, slab):
@@ -326,8 +331,7 @@
 
     def take_back(c):
         with jax.named_scope(f"waitback{c}"):
-            for k in near:
-                arrive["back", c, k].wait_recv()
+            returned[c].wait_recv()
         block = r.back[c].reshape(experts * height, features)
         r.found[...] = jnp.dot(r.sel[...], block, preferred_element_type=WIDE).astype(LOW)
 
@@ -366,54 +370,109 @@
         for c in range(chunks):
             for j in range(tensor):
                 slab = r.rows.at[c, other, around(t, -j, tensor)]
-                push(slab, slab, r.xs.at[c, j, i], r.xr.at[c, j, i], "dp", around(d, i, dp)).wait_recv()
+                push(slab, slab, r.xs.at[c, j, i - 1], r.xr.at[c, j, i - 1], "dp", around(d, i, dp)).wait_recv()
             unpack(c, other, i * full + c * group)
 
     scope = jax.named_scope
-    steps = []
 
     def step(name, action):
         with scope(name):
             action()
 
-    def turn_weight(copy, weight, turned):
-        copy.wait()
-        transpose(weight, turned)
+    def weights_ready():
+        w1_copy.wait()
+        w2_copy.wait()
+
+    def wait_image(b):
+        image_copy(b, 0).wait()
+        image_copy(b, 1).wait()
+
+    def set_gains():
+        for copy in small:
+            copy.wait()
+        r.gains[...] = jnp.concatenate([r.gain_rows[n:n + 1, :] for n in range(lanes)], axis=1)
+
+    def mix_pair(b, after):
+        if after:
+            wait_image(b + 1)
+            normalise(b + 1)
+        mix_image(b, b % pair)
+        if b % pair == pair - 1:
+            pack_rows(b // pair)
+
+    def start_mix():
+        r.mixes[...] = image_order()
+        image_copy(0, 0).wait()
+        set_gains()
+        normalise(0)
+
+    def mix_first():
+        image_copy(0, 1).wait()
+        for b in range(1, pair):
+            wait_image(b)
+        for b in range(1, pair):
+            normalise(b)
+        for b in range(pair):
+            mix_image(b, b)
+        pack_rows(0)
 
     last = chunks - 1
-    for c in range(chunks):
-        step(f"mix{c}", lambda: mix(c))
-        if c == 0:
-            step("barrier", lambda: pl.semaphore_wait(barrier, len(others)))
-        step(f"scatter{c}", lambda: scatter(c))
+    step("start", start_mix)
+    quarters = [experts // 4, experts // 2, 3 * experts // 4, experts]
+    step("mix01", mix_first)
+    for b in range(pair - 1, images):
+        c = b // pair
+        if b >= pair:
+            step(f"mix{b}", lambda: mix_pair(b, b + 1 < images))
+        if b % pair == pair - 1:
+            if c == 0:
+                step("barrier", lambda: pl.semaphore_wait(barrier, len(others)))
+            step(f"scatter{c}", lambda: scatter(c))
+            if b == pair - 1 and images > pair:
+                def more():
+                    wait_image(b + 1)
+                    normalise(b + 1)
+                step("more", more)
+        hook = b - pair
+        if 0 <= hook < len(quarters) and images > pair:
+            step(f"fwd0_{hook}", lambda: forward_rows(0, quarters[hook]))
     step("fwdrows0", lambda: forward_rows(0))
+    if chunks > 1:
+        step("fwd1_near", lambda: forward_rows(1, experts // 2))
     r.unp[...], r.turn[...], r.sel[...] = block_order(), stream_order(), back_order()
-    step("weights2", lambda: turn_weight(w2_copy, r.w2, r.w2_turned))
+    step("weights", weights_ready)
+    step("weights2", lambda: transpose(r.w2, r.w2_turned))
     if chunks > 1:
         step("fwdrows1", lambda: forward_rows(1))
-    step("weights1", lambda: turn_weight(w1_copy, r.w1, r.w1_turned))
+    if chunks > 2:
+        step("fwd2_near", lambda: forward_rows(2, experts // 2))
     for c in range(chunks):
         base = c * group
         step(f"gather{c}", lambda: gather_rows(c))
         step(f"unpack{c}", lambda: unpack(c, mine, base))
         step(f"forward{c}", lambda: forward(base, group))
         step(f"project{c}", lambda: project(c, base))
+        if c == 0:
+            step("weights1", lambda: transpose(r.w1, r.w1_turned))
+        if c > 1:
+            step(f"giveback{c - 2}", lambda: give_back(c - 2))
         if c + 2 < chunks:
             step(f"fwdrows{c + 2}", lambda: forward_rows(c + 2))
         step(f"backward{c}", lambda: backward(base, group))
         step(f"projback{c}", lambda: project_back(c, base))
-        if c > 0:
-            step(f"giveback{c - 1}", lambda: give_back(c - 1))
-    if chunks > 2:
-        step("takeback0", lambda: take_back(0))
-    for i in range(1, spread):
-        step("otherrows", lambda: other_rows(i))
-        step("otherfwd", lambda: forward(i * full, full))
-    step(f"giveback{last}", lambda: give_back(last))
-    for c in range(1 if chunks > 2 else 0, last):
+    def other_forward():
+        for i in range(1, spread):
+            step("otherrows", lambda: other_rows(i))
+            step("otherfwd", lambda: forward(i * full, full))
+
+    for c in range(max(chunks - 2, 0), chunks):
+        step(f"giveback{c}", lambda: give_back(c))
+    for c in range(last):
         step(f"takeback{c}", lambda: take_back(c))
-    for i in range(1, spread):
-        step("otherbwd", lambda: backward(i * full, full))
+        if c == 0:
+            other_forward()
+    if last == 0:
+        other_forward()
     if finish:
         width = r.gin.shape[0]
         mine_cols = pl.ds(pl.multiple_of(d * width, 128), width)
@@ -433,12 +492,6 @@
                 cols = pl.ds(pl.multiple_of(n * TILE, TILE), TILE)
                 r.gout[cols, :] = contract_rows(r.h_all[:, cols], r.g_all[:, mine_cols]).astype(LOW)
 
-        step("productin", product_in)
-    else:
-        place_out(r.s_all, r.s_out)
-        place_out(r.g_all, r.g_out)
-        place_out(r.h_all, r.h_out)
-        place_out(r.p_all, r.p_out)
     step(f"takeback{last}", lambda: take_back(last))
 
     each = r.pack.shape[1] // 8
@@ -460,16 +513,26 @@
 
     def reduce_copy(k):
         return pltpu.make_async_remote_copy(
-            src_ref=r.pack.at[rank(targets[k])], dst_ref=r.heap.at[k], send_sem=r.ss.at[k],
-            recv_sem=r.sr.at[k], device_id=targets[k], device_id_type=MESH)
+            src_ref=r.pack.at[rank(targets[k])], dst_ref=r.heap.at[k], send_sem=r.ends.at[0],
+            recv_sem=r.ends.at[1], device_id=targets[k], device_id_type=MESH)
 
     def spread_copy(k):
         return pltpu.make_async_remote_copy(
-            src_ref=r.total, dst_ref=r.summed.at[me], send_sem=r.gs.at[k],
-            recv_sem=r.gr.at[k], device_id=targets[k], device_id_type=MESH)
+            src_ref=r.total, dst_ref=r.summed.at[me], send_sem=r.ends.at[2],
+            recv_sem=r.ends.at[3], device_id=targets[k], device_id_type=MESH)
+
+    def many(size, n):
+        some = r.heap.at[pl.ds(0, size)]
+        return pltpu.make_async_remote_copy(
+            src_ref=some, dst_ref=some, send_sem=r.ends.at[n], recv_sem=r.ends.at[n + 1],
+            device_id=targets[1], device_id_type=MESH)
 
     def gated(test, action):
         pl.when(test)(action)
+
+    def by_owner(action):
+        gated(me < owners, lambda: action(owners - 1))
+        gated(me >= owners, lambda: action(owners))
 
     for k in others:
         gated(rank(targets[k]) < owners, lambda k=k: reduce_copy(k).start())
@@ -480,13 +543,14 @@
             finish_image(b)
 
     step("elem", finish_images)
+    for i in range(1, spread):
+        step("otherbwd", lambda: backward(i * full, full))
 
     def reduce_own():
         @pl.when(me < owners)
         def _():
             r.heap[0] = r.pack[me]
-            for k in others:
-                reduce_copy(k).wait_recv()
+            many(len(others), 0).wait_recv()
             r.total[...] = jnp.sum(r.heap[...], axis=0)
             for k in others:
                 spread_copy(k).start()
@@ -494,19 +558,23 @@
 
     step("reduceown", reduce_own)
     if finish:
+        step("productin", product_in)
         step("productout", product_out)
+    else:
+        place_out(r.s_all, r.s_out)
+        place_out(r.g_all, r.g_out)
+        place_out(r.h_all, r.h_out)
+        place_out(r.p_all, r.p_out)
 
     def drain():
-        for copy in started:
+        for copy in sent:
             copy.wait_send()
-        for k in others:
-            gated(rank(targets[k]) < owners, lambda k=k: reduce_copy(k).wait_send())
+        by_owner(lambda size: many(size, 0).wait_send())
 
     step("drain", drain)
 
     def collect():
-        for k in others:
-            gated(rank(sources[k]) < owners, lambda k=k: spread_copy(k).wait_recv())
+        by_owner(lambda size: many(size, 2).wait_recv())
         for n in range(bands * lanes):
             band, lane = n // lanes, n % lanes
             r.keys_out[band * 8:band * 8 + 8, lane * 128:lane * 128 + 128] = r.summed[
@@ -516,11 +584,7 @@
             row = m % each * 8 + n % 8
             r.gain_out[n:n + 1, :] = r.summed[m // each, row:row + 1, :]
 
-        @pl.when(me < owners)
-        def _():
-            for k in others:
-                spread_copy(k).wait_send()
-
+        gated(me < owners, lambda: many(len(others), 2).wait_send())
         for copy in placed:
             copy.wait()
 
@@ -584,13 +648,11 @@
         pack=vmem((devices, each * 8, 128), WIDE),
         heap=vmem((devices, each * 8, 128), WIDE), total=vmem((each * 8, 128), WIDE),
         summed=vmem((devices, each * 8, 128), WIDE),
-        in_sem=dma((8,)), image_sem=dma((2, images)), out_sem=dma((4,)),
-        zs=dma((chunks, experts)), zr=dma((chunks, experts)),
-        ys=dma((chunks, tensor, experts)), yr=dma((chunks, tensor, experts)),
-        xs=dma((chunks, tensor, spread)), xr=dma((chunks, tensor, spread)),
-        ps=dma((chunks, 2, tensor)), pr=dma((chunks, 2, tensor)),
-        bs=dma((chunks, experts)), br=dma((chunks, experts)),
-        ss=dma((devices,)), sr=dma((devices,)), gs=dma((devices,)), gr=dma((devices,)),
+        in_sem=dma((4,)), image_sem=dma((2, images)), out_sem=dma((4,)), ends=dma((4,)),
+        zs=dma((chunks,)), zr=dma((chunks, experts)), bs=dma((chunks,)), br=dma((chunks,)),
+        ys=dma((chunks, max(tensor - 1, 1))), yr=dma((chunks, max(tensor - 1, 1))),
+        xs=dma((chunks, tensor, max(spread - 1, 1))), xr=dma((chunks, tensor, max(spread - 1, 1))),
+        ps=dma((chunks, 2, max(tensor - 1, 1))), pr=dma((chunks, 2, max(tensor - 1, 1))),
     )
     if finish:
         scratch.update(turned=vmem((features // dp, total), LOW))

time: 62.3 us -> 54.6 us (0.88)
  Pallas kernels: 61.4 us -> 53.7 us
    pallas_call x1, Pallas kernels: 58.3 us -> 50.6 us  [exchange(): pl.pallas_call(functools.partial(exchange_kernel, sizes, spread, finish,...]
where the time goes in v3:
time: 54.6 us; the launch traced here: 54.5 us
  Pallas kernels  53.7 us (98%)
  between operations  0.8 us (1%)
    pallas_call x1, Pallas kernels, exchange(): pl.pallas_call(functools.partial(exchange_kernel, sizes, spread, finish,...  50.6 us
    pallas_call x1, Pallas kernels, store(): pl.pallas_call(functools.partial(store_kernel, count), out_shape=[jax.Sha...  3.08 us

profile of v3, /device:TPU:0, one launch (start us, length us, event | category | flops | bytes accessed | tf_op | source)
XLA Modules:
  0.0 54.5 jit_solution(10142324677971722474)
XLA Ops:
  0.6 50.6 %exchange.1 = (bf16[6,256,1280]{2,1,0:T(8,128)(2,1)S(1)}, f32[10,128]{1,0:T(8,128)S(1)}, f32[16,1280]{1,0:T(8,128)S(1)}, bf16[640,1280]{1,0:T(8,128)(2,1)S(1)}, bf16[1280,640]{1,0:T(8,128)(2,1)S(1)}) custom-call(bf16[6,256,1280]{2,1,0:T(8,128)(2,1)} %refs_0_.1, bf16[6,256,1280]{2,1,0:T(8,128)(2,1)} %refs_1_.1, f32[10,128]{1,0:T(8,128)} %bitcast.11, ...), custom_call_target="tpu_custom_call" | custom-call | tf_op jit(solution)/shard_map/exchange/pallas_call | solution.py:661
  51.3 3.1 %store.1 = (bf16[6,256,1280]{2,1,0:T(8,128)(2,1)}, f32[10,128]{1,0:T(8,128)}, f32[16,1280]{1,0:T(8,128)}, bf16[640,1280]{1,0:T(8,128)(2,1)}, bf16[1280,640]{1,0:T(8,128)(2,1)}) custom-call(bf16[6,256,1280]{2,1,0:T(8,128)(2,1)S(1)} %get-tuple-element.15.refs_0_, f32[10,128]{1,0:T(8,128)S(1)} %get-tuple-element.16.refs_1_, ...), custom_call_target="tpu_custom_call" | custom-call | tf_op jit(solution)/shard_map/store/pallas_call | solution.py:687

commit v4 on v3

--- a/solution.py
+++ b/solution.py
@@ -17,7 +17,7 @@
 TILE = 256
 ROWS = 64
 LOW, WIDE = jnp.bfloat16, jnp.float32
-LIMIT = 40 * 1024 * 1024
+LIMIT = 46 * 1024 * 1024
 
 
 def contract_rows(left, right):
@@ -99,12 +99,6 @@
     def columns(tile, extent=features):
         return [slice(n, n + tile) for n in range(0, extent, tile)]
 
-    sent, returned = [], {}
-
-    def launch(copy):
-        copy.start()
-        sent.append(copy)
-
     offsets = [(a, b, c) for a in range(dp) for b in range(experts) for c in range(tensor)]
     targets = [tuple(around(w, k, s) for w, k, s in zip(where, step, sizes)) for step in offsets]
     sources = [tuple(around(w, -k, s) for w, k, s in zip(where, step, sizes)) for step in offsets]
@@ -120,8 +114,9 @@
         return copy
 
     def image_copy(b, n):
+        some = b if b < pair else pl.ds(pair, images - pair)
         return pltpu.make_async_copy(
-            (r.x_in, r.c_in)[n].at[b], (r.x, r.c)[n].at[b], r.image_sem.at[n, b])
+            (r.x_in, r.c_in)[n].at[some], (r.x, r.c)[n].at[some], r.image_sem.at[n, min(b, pair)])
 
     small = [fetch(r.gain_in, r.gain_rows), fetch(r.keys_in, r.keys)]
     for b in range(pair):
@@ -130,9 +125,9 @@
     barrier = pltpu.get_barrier_semaphore()
     for k in others:
         pl.semaphore_signal(barrier, inc=1, device_id=targets[k], device_id_type=MESH)
-    for b in range(pair, images):
-        image_copy(b, 0).start()
-        image_copy(b, 1).start()
+    if images > pair:
+        image_copy(pair, 0).start()
+        image_copy(pair, 1).start()
     w1_copy, w2_copy = fetch(r.w1_in, r.w1), fetch(r.w2_in, r.w2)
     image_order, block_order, stream_order, back_order = orders(pair, experts, tensor)
     r.keys_sum[...] = jnp.zeros_like(r.keys_sum)
@@ -153,9 +148,9 @@
             r.inverse[b, rows, :] = jnp.broadcast_to(lax.rsqrt(spread_of + EPSILON), (ROWS, 128))
         for rows in blocks:
             average, inverse = r.average[b, rows, :], r.inverse[b, rows, :]
-            for lane in columns(128):
+            for n, lane in enumerate(columns(128)):
                 centred = r.x[b, rows, lane].astype(WIDE) - average
-                r.normed[b, rows, lane] = (centred * inverse * r.gains[:, lane]).astype(LOW)
+                r.normed[b, rows, lane] = (centred * inverse * r.gain_rows[n:n + 1, :]).astype(LOW)
 
     def mix_image(b, slab):
         logits = contract_cols(r.keys[...], r.normed[b])
@@ -189,45 +184,43 @@
     else:
         goes = [around(e, k, experts) for k in range(experts)]
         comes = [around(e, -k, experts) for k in range(experts)]
-    arrive = {}
+    batch = max(experts // 4, 1)
 
     def scatter(c):
         share_rows(c, r.blk.at[c, e], 0)
         for k in near:
-            arrive[c, k] = push(r.blk.at[c, goes[k]], r.rows.at[c, mine, t, e],
-                                r.zs.at[c], r.zr.at[c, k], "expert", goes[k])
-            arrive[c, k].start()
-        most = r.rows.at[c, mine, t, pl.ds(0, experts - 1)]
-        sent.append(push(most, most, r.zs.at[c], r.zr.at[c, 1], "expert", goes[1]))
+            push(r.blk.at[c, goes[k]], r.rows.at[c, mine, t, e],
+                 r.zs.at[0], r.zr.at[c, k // batch], "expert", goes[k]).start()
         r.rows[c, mine, t, e] = r.blk[c, e]
 
     def share_rows(c, src, k):
         slot = r.rows.at[c, mine, t, comes[k]]
         for j in range(1, tensor):
-            push(src, slot, r.ys.at[c, j - 1], r.yr.at[c, j - 1], "tensor", around(t, j, tensor)).start()
+            push(src, slot, r.ys.at[j - 1], r.yr.at[c, j - 1], "tensor", around(t, j, tensor)).start()
 
     def share_slab(c, j):
         for i in range(1, spread):
             slab = r.rows.at[c, mine, around(t, -j, tensor)]
-            launch(push(slab, slab, r.xs.at[c, j, i - 1], r.xr.at[c, j, i - 1], "dp", around(d, i, dp)))
+            push(slab, slab, r.xs.at[i - 1], r.xr.at[i - 1], "dp", around(d, i, dp)).start()
 
     waiting = {}
 
     def forward_rows(c, upto=experts):
         ready = [k for k in waiting.setdefault(c, list(near)) if k < upto]
-        for k in ready:
-            waiting[c].remove(k)
-            arrive[c, k].wait_recv()
-            share_rows(c, r.rows.at[c, mine, t, comes[k]], k)
+        for n in sorted({k // batch for k in ready}):
+            some = [k for k in near if k // batch == n]
+            slabs = r.rows.at[c, mine, t, pl.ds(0, len(some))]
+            push(slabs, slabs, r.zs.at[0], r.zr.at[c, n], "expert", goes[1]).wait_recv()
+            for k in some:
+                waiting[c].remove(k)
+                share_rows(c, r.rows.at[c, mine, t, comes[k]], k)
         if ready and not waiting[c]:
             share_slab(c, 0)
 
     def gather_rows(c):
         for j in range(1, tensor):
             slab = r.rows.at[c, mine, around(t, -j, tensor)]
-            whole = push(slab, slab, r.ys.at[c, j - 1], r.yr.at[c, j - 1], "tensor", around(t, j, tensor))
-            whole.wait_recv()
-            sent.append(whole)
+            push(slab, slab, r.ys.at[j - 1], r.yr.at[c, j - 1], "tensor", around(t, j, tensor)).wait_recv()
             share_slab(c, j)
 
     def unpack(c, place, base):
@@ -257,45 +250,53 @@
             x = jnp.dot(r.g_all[base:base + size, :], r.w2_turned[:, cols], preferred_element_type=WIDE)
             r.p_all[base:base + size, cols] = (x * gelu_slope(r.pre[0:size, cols])).astype(LOW)
 
-    def project(c, base):
-        for cols in columns(TILE):
+    middle = -(-features // (2 * TILE)) * TILE
+    whole = [slice(0, features)]
+    halves = {c: whole for c in range(chunks)}
+    if chunks > 2 and middle < features:
+        halves[0] = halves[chunks - 1] = [slice(0, middle), slice(middle, features)]
+
+    def tiles(span):
+        return [slice(n, min(n + TILE, span.stop)) for n in range(span.start, span.stop, TILE)]
+
+    def project(c, base, half=0):
+        for cols in tiles(halves[c][half]):
             r.part[c, 0, :, cols] = jnp.dot(
                 r.h_all[base:base + group, :], r.w2[:, cols], preferred_element_type=WIDE)
-        share_part(c, 0)
-
-    def project_back(c, base):
-        for cols in columns(TILE):
-            r.part[c, 1, :, cols] = jnp.dot(
-                r.p_all[base:base + group, :], r.w1_turned[:, cols], preferred_element_type=WIDE)
-        share_part(c, 1)
-
-    def part_copy(c, which, j):
-        return push(r.sent.at[c, which, j - 1], r.got.at[c, which, j - 1],
-                    r.ps.at[c, which, j - 1], r.pr.at[c, which, j - 1], "tensor", around(t, j, tensor))
-
-    def share_part(c, which):
+        share_part(c, 0, half)
+
+    def project_back(c, base, half=0):
+        for cols in tiles(halves[c][half]):
+            r.part[c, 1, :, cols] = contract_cols(r.p_all[base:base + group, :], r.w1[cols, :])
+        share_part(c, 1, half)
+
+    def share_part(c, which, half):
+        cols = halves[c][half]
         for j in range(1, tensor):
             to = around(t, j, tensor)
-            r.sent[c, which, j - 1] = r.part[c, which, pl.ds(pl.multiple_of(to * own, 8), own), :].astype(LOW)
-            launch(part_copy(c, which, j))
-
-    def give_back(c):
+            r.sent[c, which, j - 1, :, cols] = r.part[
+                c, which, pl.ds(pl.multiple_of(to * own, 8), own), cols].astype(LOW)
+            push(r.sent.at[c, which, j - 1, :, cols], r.got.at[c, which, j - 1, :, cols],
+                 r.ps.at[0], r.pr.at[c, half], "tensor", to).start()
+
+    def give_back(c, half=0):
+        cols = halves[c][half]
         totals = []
+        if tensor > 1:
+            both = r.got.at[c, :, :, :, cols]
+            push(both, both, r.ps.at[0], r.pr.at[c, half], "tensor", around(t, 1, tensor)).wait_recv()
         for which in range(2):
-            total = r.part[c, which, pl.ds(pl.multiple_of(t * own, 8), own), :]
+            total = r.part[c, which, pl.ds(pl.multiple_of(t * own, 8), own), cols]
             for j in range(1, tensor):
-                part_copy(c, which, j).wait_recv()
-                total = total + r.got[c, which, j - 1].astype(WIDE)
+                total = total + r.got[c, which, j - 1, :, cols].astype(WIDE)
             totals.append(total.astype(LOW))
         moved = jnp.dot(r.turn[...], jnp.concatenate(totals, axis=0), preferred_element_type=WIDE)
         for n in range(experts):
-            r.ret[c, n] = moved[n * height:(n + 1) * height].astype(LOW)
+            r.ret[c, n, :, cols] = moved[n * height:(n + 1) * height].astype(LOW)
         for k in reversed(near):
-            push(r.ret.at[c, goes[k]], r.back.at[c, e], r.bs.at[c], r.br.at[c], "expert", goes[k]).start()
-        most = r.back.at[c, pl.ds(0, experts - 1)]
-        returned[c] = push(most, most, r.bs.at[c], r.br.at[c], "expert", goes[1])
-        sent.append(returned[c])
-        r.back[c, e] = r.ret[c, e]
+            push(r.ret.at[c, goes[k], :, cols], r.back.at[c, e, :, cols],
+                 r.bs.at[0], r.br.at[c, half], "expert", goes[k]).start()
+        r.back[c, e, :, cols] = r.ret[c, e, :, cols]
 
     def image_gradients(b, slab):
         start = slab * 2 * slots
@@ -331,7 +332,9 @@
 
     def take_back(c):
         with jax.named_scope(f"waitback{c}"):
-            returned[c].wait_recv()
+            for half, cols in enumerate(halves[c]):
+                most = r.back.at[c, pl.ds(0, experts - 1), :, cols]
+                push(most, most, r.bs.at[0], r.br.at[c, half], "expert", goes[1]).wait_recv()
         block = r.back[c].reshape(experts * height, features)
         r.found[...] = jnp.dot(r.sel[...], block, preferred_element_type=WIDE).astype(LOW)
 
@@ -367,10 +370,9 @@
 
     def other_rows(i):
         other = around(d, -i, dp)
+        slabs = r.rows.at[:, other]
+        push(slabs, slabs, r.xs.at[i - 1], r.xr.at[i - 1], "dp", around(d, i, dp)).wait_recv()
         for c in range(chunks):
-            for j in range(tensor):
-                slab = r.rows.at[c, other, around(t, -j, tensor)]
-                push(slab, slab, r.xs.at[c, j, i - 1], r.xr.at[c, j, i - 1], "dp", around(d, i, dp)).wait_recv()
             unpack(c, other, i * full + c * group)
 
     scope = jax.named_scope
@@ -384,12 +386,11 @@
         w2_copy.wait()
 
     def wait_image(b):
-        image_copy(b, 0).wait()
-        image_copy(b, 1).wait()
+        if b <= pair:
+            image_copy(b, 0).wait()
+            image_copy(b, 1).wait()
 
     def set_gains():
-        for copy in small:
-            copy.wait()
         r.gains[...] = jnp.concatenate([r.gain_rows[n:n + 1, :] for n in range(lanes)], axis=1)
 
     def mix_pair(b, after):
@@ -403,7 +404,8 @@
     def start_mix():
         r.mixes[...] = image_order()
         image_copy(0, 0).wait()
-        set_gains()
+        for copy in small:
+            copy.wait()
         normalise(0)
 
     def mix_first():
@@ -418,7 +420,7 @@
 
     last = chunks - 1
     step("start", start_mix)
-    quarters = [experts // 4, experts // 2, 3 * experts // 4, experts]
+    quarters = [n * batch for n in range(1, experts // batch + 1)]
     step("mix01", mix_first)
     for b in range(pair - 1, images):
         c = b // pair
@@ -438,60 +440,77 @@
             step(f"fwd0_{hook}", lambda: forward_rows(0, quarters[hook]))
     step("fwdrows0", lambda: forward_rows(0))
     if chunks > 1:
-        step("fwd1_near", lambda: forward_rows(1, experts // 2))
+        step("fwd1_near", lambda: forward_rows(1, quarters[len(quarters) // 2 - 1]))
     r.unp[...], r.turn[...], r.sel[...] = block_order(), stream_order(), back_order()
+    set_gains()
     step("weights", weights_ready)
     step("weights2", lambda: transpose(r.w2, r.w2_turned))
     if chunks > 1:
         step("fwdrows1", lambda: forward_rows(1))
     if chunks > 2:
-        step("fwd2_near", lambda: forward_rows(2, experts // 2))
+        step("fwd2_near", lambda: forward_rows(2, quarters[len(quarters) // 2 - 1]))
     for c in range(chunks):
         base = c * group
         step(f"gather{c}", lambda: gather_rows(c))
         step(f"unpack{c}", lambda: unpack(c, mine, base))
         step(f"forward{c}", lambda: forward(base, group))
+        if c > 1:
+            step(f"giveback{c - 2}", lambda: give_back(c - 2, len(halves[c - 2]) - 1))
         step(f"project{c}", lambda: project(c, base))
-        if c == 0:
-            step("weights1", lambda: transpose(r.w1, r.w1_turned))
-        if c > 1:
-            step(f"giveback{c - 2}", lambda: give_back(c - 2))
+        step(f"backward{c}", lambda: backward(base, group))
+        if c == 1 and len(halves[0]) > 1:
+            step("giveback0a", lambda: give_back(0))
+        step(f"projback{c}", lambda: project_back(c, base))
         if c + 2 < chunks:
             step(f"fwdrows{c + 2}", lambda: forward_rows(c + 2))
-        step(f"backward{c}", lambda: backward(base, group))
-        step(f"projback{c}", lambda: project_back(c, base))
+        for half in range(1, len(halves[c])):
+            step(f"project{c}", lambda: project(c, base, half))
+            step(f"projback{c}", lambda: project_back(c, base, half))
+
+    if finish:
+        width = r.gin.shape[0]
+        mine_cols = pl.ds(pl.multiple_of(d * width, 128), width)
+
+    def add_up(i, total, out, place, value):
+        if i > 0:
+            value = value + total[place]
+        if i == spread - 1:
+            out[place] = value.astype(LOW)
+        else:
+            total[place] = value
+
+    def product_in(i):
+        rows = slice(i * full, (i + 1) * full)
+        r.turned[...] = r.s_all[rows, mine_cols].T
+
+        @pl.loop(0, units // TILE)
+        def _(n):
+            cols = pl.ds(pl.multiple_of(n * TILE, TILE), TILE)
+            add_up(i, r.gin_sum, r.gin, (slice(None), cols), jnp.dot(
+                r.turned[...], r.p_all[rows, cols], preferred_element_type=WIDE))
+
+    def product_out():
+        @pl.loop(0, units // TILE)
+        def _(n):
+            cols = pl.ds(pl.multiple_of(n * TILE, TILE), TILE)
+            r.gout[cols, :] = contract_rows(r.h_all[:, cols], r.g_all[:, mine_cols]).astype(LOW)
+
     def other_forward():
         for i in range(1, spread):
             step("otherrows", lambda: other_rows(i))
             step("otherfwd", lambda: forward(i * full, full))
 
     for c in range(max(chunks - 2, 0), chunks):
-        step(f"giveback{c}", lambda: give_back(c))
+        if finish and c == last:
+            step("ownin", lambda: product_in(0))
+        for half in range(len(halves[c])):
+            step(f"giveback{c}_{half}", lambda: give_back(c, half))
     for c in range(last):
         step(f"takeback{c}", lambda: take_back(c))
         if c == 0:
             other_forward()
     if last == 0:
         other_forward()
-    if finish:
-        width = r.gin.shape[0]
-        mine_cols = pl.ds(pl.multiple_of(d * width, 128), width)
-
-        def product_in():
-            r.turned[...] = r.s_all[:, mine_cols].T
-
-            @pl.loop(0, units // TILE)
-            def _(n):
-                cols = pl.ds(pl.multiple_of(n * TILE, TILE), TILE)
-                r.gin[:, cols] = jnp.dot(
-                    r.turned[...], r.p_all[:, cols], preferred_element_type=WIDE).astype(LOW)
-
-        def product_out():
-            @pl.loop(0, units // TILE)
-            def _(n):
-                cols = pl.ds(pl.multiple_of(n * TILE, TILE), TILE)
-                r.gout[cols, :] = contract_rows(r.h_all[:, cols], r.g_all[:, mine_cols]).astype(LOW)
-
     step(f"takeback{last}", lambda: take_back(last))
 
     each = r.pack.shape[1] // 8
@@ -505,11 +524,11 @@
         band, lane = n // lanes, n % lanes
         r.pack[n // each, pl.ds(n % each * 8, 8), :] = r.keys_sum[
             band * 8:band * 8 + 8, lane * 128:lane * 128 + 128]
-    for n in range(-(-lanes // 8) * 8):
+    blank = jnp.zeros((1, 128), WIDE)
+    for n in range(0, lanes, 8):
         m = bands * lanes + n // 8
-        row = m % each * 8 + n % 8
-        piece = gain[:, n * 128:n * 128 + 128] if n < lanes else jnp.zeros((1, 128), WIDE)
-        r.pack[m // each, row:row + 1, :] = piece
+        pieces = [gain[:, k * 128:k * 128 + 128] if k < lanes else blank for k in range(n, n + 8)]
+        r.pack[m // each, m % each * 8:m % each * 8 + 8, :] = jnp.concatenate(pieces, axis=0)
 
     def reduce_copy(k):
         return pltpu.make_async_remote_copy(
@@ -522,7 +541,7 @@
             recv_sem=r.ends.at[3], device_id=targets[k], device_id_type=MESH)
 
     def many(size, n):
-        some = r.heap.at[pl.ds(0, size)]
+        some = (r.heap if n == 0 else r.summed).at[pl.ds(0, size)]
         return pltpu.make_async_remote_copy(
             src_ref=some, dst_ref=some, send_sem=r.ends.at[n], recv_sem=r.ends.at[n + 1],
             device_id=targets[1], device_id_type=MESH)
@@ -543,22 +562,23 @@
             finish_image(b)
 
     step("elem", finish_images)
-    for i in range(1, spread):
-        step("otherbwd", lambda: backward(i * full, full))
 
     def reduce_own():
         @pl.when(me < owners)
         def _():
             r.heap[0] = r.pack[me]
             many(len(others), 0).wait_recv()
-            r.total[...] = jnp.sum(r.heap[...], axis=0)
+            r.total[...] = jnp.sum(r.heap[...], axis=0).astype(LOW)
             for k in others:
                 spread_copy(k).start()
             r.summed[me] = r.total[...]
 
     step("reduceown", reduce_own)
+    for i in range(1, spread):
+        step("otherbwd", lambda: backward(i * full, full))
     if finish:
-        step("productin", product_in)
+        for i in range(1, spread):
+            step("productin", lambda: product_in(i))
         step("productout", product_out)
     else:
         place_out(r.s_all, r.s_out)
@@ -567,8 +587,17 @@
         place_out(r.p_all, r.p_out)
 
     def drain():
-        for copy in sent:
-            copy.wait_send()
+        def sent(src, semaphore):
+            push(src, src, semaphore, r.zr.at[0, 0], "expert", goes[1]).wait_send()
+
+        sent(r.rows.at[:, mine, t, pl.ds(0, experts - 1)], r.zs.at[0])
+        sent(r.back.at[:, pl.ds(0, experts - 1)], r.bs.at[0])
+        if tensor > 1:
+            sent(r.got, r.ps.at[0])
+        for j in range(1, tensor):
+            sent(r.rows.at[:, mine, t], r.ys.at[j - 1])
+        for i in range(1, spread):
+            sent(r.rows.at[:, mine], r.xs.at[i - 1])
         by_owner(lambda size: many(size, 0).wait_send())
 
     step("drain", drain)
@@ -578,11 +607,11 @@
         for n in range(bands * lanes):
             band, lane = n // lanes, n % lanes
             r.keys_out[band * 8:band * 8 + 8, lane * 128:lane * 128 + 128] = r.summed[
-                n // each, n % each * 8:n % each * 8 + 8, :]
-        for n in range(lanes):
-            m = bands * lanes + n // 8
-            row = m % each * 8 + n % 8
-            r.gain_out[n:n + 1, :] = r.summed[m // each, row:row + 1, :]
+                n // each, n % each * 8:n % each * 8 + 8, :].astype(WIDE)
+        for n in range(0, lanes, 8):
+            m, some = bands * lanes + n // 8, min(8, lanes - n)
+            whole = r.summed[m // each, m % each * 8:m % each * 8 + 8, :].astype(WIDE)
+            r.gain_out[n:n + some, :] = whole[0:some]
 
         gated(me < owners, lambda: many(len(others), 2).wait_send())
         for copy in placed:
@@ -628,7 +657,7 @@
         turn=vmem((rows, rows), LOW), sel=vmem((rows, rows), LOW),
         average=vmem((images, count, 128), WIDE), inverse=vmem((images, count, 128), WIDE),
         cols=vmem((2, count, 128), WIDE),
-        w1_turned=vmem(w1.shape[::-1], LOW), w2_turned=vmem(w2.shape[::-1], LOW),
+        w2_turned=vmem(w2.shape[::-1], LOW),
         logits=vmem((images, slots, count), WIDE), disp=vmem((images, slots, count), WIDE),
         comb=vmem((images, slots, count), WIDE), slot_in=vmem((images, slots, features), WIDE),
         stack=vmem((2 * pair * slots, features), LOW), found=vmem((2 * pair * slots, features), LOW),
@@ -646,16 +675,17 @@
         moment=vmem((images, 8, count), WIDE),
         keys_sum=vmem((slots, features), WIDE), gain_sum=vmem((slots, features), WIDE),
         pack=vmem((devices, each * 8, 128), WIDE),
-        heap=vmem((devices, each * 8, 128), WIDE), total=vmem((each * 8, 128), WIDE),
-        summed=vmem((devices, each * 8, 128), WIDE),
-        in_sem=dma((4,)), image_sem=dma((2, images)), out_sem=dma((4,)), ends=dma((4,)),
-        zs=dma((chunks,)), zr=dma((chunks, experts)), bs=dma((chunks,)), br=dma((chunks,)),
-        ys=dma((chunks, max(tensor - 1, 1))), yr=dma((chunks, max(tensor - 1, 1))),
-        xs=dma((chunks, tensor, max(spread - 1, 1))), xr=dma((chunks, tensor, max(spread - 1, 1))),
-        ps=dma((chunks, 2, max(tensor - 1, 1))), pr=dma((chunks, 2, max(tensor - 1, 1))),
+        heap=vmem((devices, each * 8, 128), WIDE), total=vmem((each * 8, 128), LOW),
+        summed=vmem((devices, each * 8, 128), LOW),
+        in_sem=dma((4,)), image_sem=dma((2, pair + 1)), out_sem=dma((1 if finish else 4,)), ends=dma((4,)),
+        zs=dma((1,)), zr=dma((chunks, experts // max(experts // 4, 1))), bs=dma((1,)), br=dma((chunks, 2)),
+        ys=dma((max(tensor - 1, 1),)), yr=dma((chunks, max(tensor - 1, 1))),
+        xs=dma((max(spread - 1, 1),)), xr=dma((max(spread - 1, 1),)),
+        ps=dma((1,)), pr=dma((chunks, 2)),
     )
     if finish:
-        scratch.update(turned=vmem((features // dp, total), LOW))
+        scratch.update(turned=vmem((features // dp, total // spread), LOW),
+                       gin_sum=vmem((features // dp, units), WIDE))
     far, near = pl.BlockSpec(memory_space=pltpu.HBM), pl.BlockSpec(memory_space=vmem)
     names = list(ins) + list(outs) + list(scratch)
     values = pl.pallas_call(
@@ -665,7 +695,7 @@
         out_specs=[near] * held + [far] * (len(outs) - held),
         scratch_shapes=list(scratch.values()),
         compiler_params=pltpu.CompilerParams(
-            collective_id=0, has_side_effects=True, vmem_limit_bytes=LIMIT if finish else LIMIT + LIMIT // 4
+            collective_id=0, has_side_effects=True, vmem_limit_bytes=LIMIT if finish else LIMIT + LIMIT // 8
         ),
         name="exchange",
     )(*[pltpu.with_memory_space_constraint(v, pltpu.HBM) for v in ins.values()])

time: 54.6 us -> 54.1 us (level)
  no operation moved by 1% of the time
where the time goes in v4:
time: 54.1 us; the launch traced here: 54 us
  Pallas kernels  53.2 us (98%)
  between operations  0.8 us (1%)
    pallas_call x1, Pallas kernels, exchange(): pl.pallas_call(functools.partial(exchange_kernel, sizes, spread, finish,...  50.1 us
    pallas_call x1, Pallas kernels, store(): pl.pallas_call(functools.partial(store_kernel, count), out_shape=[jax.Sha...  3.08 us

profile of v4, /device:TPU:0, one launch (start us, length us, event | category | flops | bytes accessed | tf_op | source)
XLA Modules:
  0.0 54.0 jit_solution(12930291845897075009)
XLA Ops:
  0.6 50.1 %exchange.1 = (bf16[6,256,1280]{2,1,0:T(8,128)(2,1)S(1)}, f32[10,128]{1,0:T(8,128)S(1)}, f32[16,1280]{1,0:T(8,128)S(1)}, bf16[640,1280]{1,0:T(8,128)(2,1)S(1)}, bf16[1280,640]{1,0:T(8,128)(2,1)S(1)}) custom-call(bf16[6,256,1280]{2,1,0:T(8,128)(2,1)} %refs_0_.1, bf16[6,256,1280]{2,1,0:T(8,128)(2,1)} %refs_1_.1, f32[10,128]{1,0:T(8,128)} %bitcast.11, ...), custom_call_target="tpu_custom_call" | custom-call | tf_op jit(solution)/shard_map/exchange/pallas_call | solution.py:691
  50.7 3.1 %store.1 = (bf16[6,256,1280]{2,1,0:T(8,128)(2,1)}, f32[10,128]{1,0:T(8,128)}, f32[16,1280]{1,0:T(8,128)}, bf16[640,1280]{1,0:T(8,128)(2,1)}, bf16[1280,640]{1,0:T(8,128)(2,1)}) custom-call(bf16[6,256,1280]{2,1,0:T(8,128)(2,1)S(1)} %get-tuple-element.15.refs_0_, f32[10,128]{1,0:T(8,128)S(1)} %get-tuple-element.16.refs_1_, ...), custom_call_target="tpu_custom_call" | custom-call | tf_op jit(solution)/shard_map/store/pallas_call | solution.py:717

commit v5 on v4

--- a/solution.py
+++ b/solution.py
@@ -3,6 +3,7 @@
 
 import jax
 import jax.numpy as jnp
+import numpy as np
 from jax import lax
 from jax.experimental import pallas as pl
 from jax.experimental.pallas import tpu as pltpu
@@ -706,8 +707,14 @@
     copies = [
         pltpu.make_async_copy(refs[n], refs[count + n], refs[-1].at[n]) for n in range(count)
     ]
-    for copy in copies:
-        copy.start()
+    order = sorted(range(count), key=lambda n: -np.prod(refs[n].shape))
+    for n in order:
+        size = refs[n].shape[0]
+        parts = size if len(refs[n].shape) == 3 else 4 if size % 32 == 0 else 1
+        for m in range(parts):
+            some = pl.ds(m * (size // parts), size // parts)
+            pltpu.make_async_copy(
+                refs[n].at[some], refs[count + n].at[some], refs[-1].at[n]).start()
     for copy in copies:
         copy.wait()
 

time: 54.1 us -> 54 us (level)
  no operation moved by 1% of the time
where the time goes in v5:
time: 54 us; the launch traced here: 53.9 us
  Pallas kernels  53.1 us (98%)
  between operations  0.8 us (1%)
    pallas_call x1, Pallas kernels, exchange(): pl.pallas_call(functools.partial(exchange_kernel, sizes, spread, finish,...  50.1 us
    pallas_call x1, Pallas kernels, store(): pl.pallas_call(functools.partial(store_kernel, count), out_shape=[jax.Sha...  2.98 us

profile of v5, /device:TPU:0, one launch (start us, length us, event | category | flops | bytes accessed | tf_op | source)
XLA Modules:
  0.0 53.9 jit_solution(12745347587420369988)
XLA Ops:
  0.6 50.1 %exchange.1 = (bf16[6,256,1280]{2,1,0:T(8,128)(2,1)S(1)}, f32[10,128]{1,0:T(8,128)S(1)}, f32[16,1280]{1,0:T(8,128)S(1)}, bf16[640,1280]{1,0:T(8,128)(2,1)S(1)}, bf16[1280,640]{1,0:T(8,128)(2,1)S(1)}) custom-call(bf16[6,256,1280]{2,1,0:T(8,128)(2,1)} %refs_0_.1, bf16[6,256,1280]{2,1,0:T(8,128)(2,1)} %refs_1_.1, f32[10,128]{1,0:T(8,128)} %bitcast.11, ...), custom_call_target="tpu_custom_call" | custom-call | tf_op jit(solution)/shard_map/exchange/pallas_call | solution.py:692
  50.7 3.0 %store.1 = (bf16[6,256,1280]{2,1,0:T(8,128)(2,1)}, f32[10,128]{1,0:T(8,128)}, f32[16,1280]{1,0:T(8,128)}, bf16[640,1280]{1,0:T(8,128)(2,1)}, bf16[1280,640]{1,0:T(8,128)(2,1)}) custom-call(bf16[6,256,1280]{2,1,0:T(8,128)(2,1)S(1)} %get-tuple-element.15.refs_0_, f32[10,128]{1,0:T(8,128)S(1)} %get-tuple-element.16.refs_1_, ...), custom_call_target="tpu_custom_call" | custom-call | tf_op jit(solution)/shard_map/store/pallas_call | solution.py:724
